TPU v7x, 8 devices: a whole 2x2x1 slice. The times are simulated.
8 devices in a mesh: part: 1 (over z), col: 2 (over y), row: 4 (over x, core).
Axes of the slice: x: 2, y: 2, z: 1, core: 2. Of those that a mesh axis runs over, the one named last changes fastest.
Arguments:
- l_in: float32 [192, 64, 12288], P(('part', 'row'), None, 'col')
Outputs:
- output 1: float32 [192, 64, 12288], P(('part', 'row'), None, 'col')
- output 2: float32 [4, 128, 64], P('part')
- output 3: float32 [4, 12288, 64], P(None, ('part', 'row'))
- output 4: float32 [4, 64, 64], P('part')
All inputs are finite; a program needn't handle non-finite values.
Results may differ from a plain program's by a relative error of at most 0.001.
Values sent between devices are 32-bit elements.
A program may use at most 1 GiB of HBM per device.

v0:
```python
import jax
import jax.numpy as jnp
from jax import lax
from jax.sharding import PartitionSpec as P

PANELS = 4
PREC_HIGH = lax.Precision.HIGHEST


def mat_dot(left, right):
    return jnp.dot(left, right, precision=PREC_HIGH, preferred_element_type=jnp.float32)


def dot_tn(left, right):
    return lax.dot_general(left, right, (((0,), (0,)), ((), ())), precision=PREC_HIGH, preferred_element_type=jnp.float32)


def dot_nt(left, right):
    return lax.dot_general(left, right, (((1,), (1,)), ((), ())), precision=PREC_HIGH, preferred_element_type=jnp.float32)


def triangular_factor(tau_vec, gram):
    block = gram.shape[0]
    col_ids = jnp.arange(block)

    def t_column(col_idx, tri_mat):
        g_col = jnp.where(col_ids < col_idx, lax.dynamic_index_in_dim(gram, col_idx, axis=1, keepdims=False), 0.0)
        tau_val = lax.dynamic_index_in_dim(tau_vec, col_idx, keepdims=False)
        new_col = jnp.where(col_ids == col_idx, tau_val, -tau_val * jnp.dot(tri_mat, g_col, precision=PREC_HIGH, preferred_element_type=jnp.float32))
        return jnp.where((col_ids == col_idx)[None, :], new_col[:, None], tri_mat)

    return lax.fori_loop(0, block, t_column, jnp.zeros((block, block), jnp.float32))


def panel_qr(panel, rel_row):
    block = panel.shape[1]
    col_ids = jnp.arange(block)

    def qr_column(col_idx, carry):
        work, vecs, tau_vec = carry
        column = lax.dynamic_index_in_dim(work, col_idx, axis=1, keepdims=False)
        below = jnp.where(rel_row >= col_idx, column, 0.0)
        head = jnp.sum(jnp.where(rel_row == col_idx, column, 0.0))
        stats = lax.psum(jnp.stack([head, jnp.sum(below * below)]), "row")
        alpha_val = stats[0]
        norm_x = jnp.sqrt(stats[1])
        beta_val = jnp.where(alpha_val >= 0.0, -norm_x, norm_x)
        tau_val = (beta_val - alpha_val) / beta_val
        house = jnp.where(rel_row == col_idx, 1.0, jnp.where(rel_row > col_idx, below / (alpha_val - beta_val), 0.0))
        proj = lax.psum(jnp.dot(house, work, precision=PREC_HIGH, preferred_element_type=jnp.float32), "row")
        proj = jnp.where(col_ids > col_idx, proj, 0.0)
        work = work - tau_val * house[:, None] * proj[None, :]
        new_col = jnp.where(rel_row < col_idx, column, jnp.where(rel_row == col_idx, beta_val, 0.0))
        pick = (col_ids == col_idx)[None, :]
        work = jnp.where(pick, new_col[:, None], work)
        vecs = jnp.where(pick, house[:, None], vecs)
        tau_vec = jnp.where(col_ids == col_idx, tau_val, tau_vec)
        return work, vecs, tau_vec

    begin = (panel, jnp.zeros_like(panel), jnp.zeros((block,), jnp.float32))
    return lax.fori_loop(0, block, qr_column, begin)


def solution(mesh):
    proc_rows = mesh.shape["row"]
    proc_cols = mesh.shape["col"]
    mat_spec = P(("part", "row"), None, "col")

    def local_step(l_blk):
        row_blocks, block, cols_loc = l_blk.shape
        rows_loc = row_blocks * block
        col_blocks = cols_loc // block
        my_row = lax.axis_index("row")
        my_col = lax.axis_index("col")
        within = jnp.arange(block)
        row_glob = ((my_row + jnp.arange(row_blocks) * proc_rows)[:, None] * block + within[None, :]).reshape(rows_loc)
        col_glob = ((my_col + jnp.arange(col_blocks) * proc_cols)[:, None] * block + within[None, :]).reshape(cols_loc)
        strict_low = row_glob[:, None] > col_glob[None, :]
        on_diag = row_glob[:, None] == col_glob[None, :]

        def rows_to_cols(x_rows):
            blk_ids = my_col + jnp.arange(col_blocks) * proc_cols
            picked = jnp.take(x_rows.reshape(row_blocks, block, block), blk_ids // proc_rows, axis=0)
            picked = jnp.where((blk_ids % proc_rows == my_row)[:, None, None], picked, 0.0)
            return lax.psum(picked.reshape(cols_loc, block), "row")

        def cols_to_rows(x_cols):
            blk_ids = my_row + jnp.arange(row_blocks) * proc_rows
            picked = jnp.take(x_cols.reshape(col_blocks, block, block), blk_ids // proc_cols, axis=0)
            picked = jnp.where((blk_ids % proc_cols == my_col)[:, None, None], picked, 0.0)
            return lax.psum(picked.reshape(rows_loc, block), "col")

        half_mat = jnp.where(on_diag, 0.5, 1.0) * l_blk.reshape(rows_loc, cols_loc)
        band_list = []
        vec_list = []
        tri_list = []
        for panel_idx in range(PANELS):
            start = panel_idx * block
            rel_row = row_glob - (start + block)
            in_trail = (rel_row >= 0)[:, None]
            col_slot = (panel_idx // proc_cols) * block
            col_block = half_mat[:, col_slot:col_slot + block]
            col_block = lax.psum(jnp.where(my_col == panel_idx % proc_cols, col_block, 0.0), "col")
            reduced, vecs, tau_vec = panel_qr(jnp.where(in_trail, col_block, 0.0), rel_row)
            t_mat = triangular_factor(tau_vec, lax.psum(dot_tn(vecs, vecs), "row"))
            diag_pick = (row_glob[None, :] - start == within[:, None]).astype(jnp.float32)
            r_pick = (rel_row[None, :] == within[:, None]).astype(jnp.float32)
            band_part = jnp.concatenate([mat_dot(diag_pick, col_block) * (1.0 + jnp.eye(block, dtype=jnp.float32)), mat_dot(r_pick, reduced)], axis=0)
            band_list.append(lax.psum(band_part, "row"))
            vecs_cols = rows_to_cols(vecs)
            sum_lv = lax.psum(mat_dot(half_mat, vecs_cols), "col")
            sum_ltv = lax.psum(dot_tn(half_mat, vecs), "row")
            y_rows = jnp.where(in_trail, mat_dot(sum_lv + cols_to_rows(sum_ltv), t_mat), 0.0)
            m_mat = dot_tn(t_mat, lax.psum(dot_tn(vecs, y_rows), "row"))
            w_rows = y_rows - 0.5 * mat_dot(vecs, m_mat)
            w_cols = rows_to_cols(w_rows)
            update = dot_nt(jnp.concatenate([vecs, w_rows], axis=1), jnp.concatenate([w_cols, vecs_cols], axis=1))
            half_mat = half_mat - jnp.where(strict_low, update, jnp.where(on_diag, 0.5 * update, 0.0))
            vec_list.append(vecs)
            tri_list.append(t_mat)
        done_rows = PANELS * block
        keep = (row_glob[:, None] >= done_rows) & (col_glob[None, :] >= done_rows)
        l_out = jnp.where(keep, jnp.where(on_diag, 2.0, 1.0) * half_mat, 0.0)
        return l_out.reshape(row_blocks, block, cols_loc), jnp.stack(band_list), jnp.stack(vec_list), jnp.stack(tri_list)

    return jax.shard_map(local_step, mesh=mesh, in_specs=(mat_spec,), out_specs=(mat_spec, P("part"), P(None, ("part", "row"), None), P("part")), check_vma=False)
```

profile of v0, /device:TPU:0, one launch (start us, length us, event | category | flops | bytes accessed | tf_op | source)
XLA Modules:
  0.0 7459.0 jit_solution(2833301335805700591)
XLA Ops:
  7.5 73.0 copy.31
  80.6 49.6 fusion.86
  132.9 30.8 all-reduce.23.cloned.1.call-done
  165.0 1185.3 %while.136 = (s32[]{:T(128)}, f32[3072,64]{0,1:T(8,128)S(1)}, f32[3072,64]{0,1:T(8,128)S(1)}, f32[64]{0:T(128)S(1)}, s32[48]{0:T(128)S(1)}, /*index=5*/s32[]{:T(128)}, f32[]{:T(128)}, s32[]{:T(128)}) while((s32[]{:T(128)}, f32[3072,64]{0,1:T(8,128)S(1)}, f32[3072,64]{0,1:T(8,128)S(1)}, f32[64]{0:T(128)S(1)}, ...), condition=%wide.region_6.7_spmd.clone.clone, body=%wide.region_1.6_spmd.clone.clone.sunk | while | flops 3416523 | bytes 4199006 | solution.py:61
  278.1 6.5 psum.404
  444.8 6.5 psum.404
  611.4 6.5 psum.404
  778.0 6.5 psum.404
  1111.3 6.5 psum.404
  1350.7 64.1 fusion.137
  1425.4 11.9 psum.345
  1437.4 76.5 %all-reduce.55.cloned.1.call-done = (f32[6144,64]{0,1:T(8,128)}, f32[96,64,64]{2,1,0:T(8,128)}) async-done(((f32[6144,64]{0,1:T(8,128)}, f32[96,64,64]{2,1,0:T(8,128)}), (f32[6144,64]{0,1:T(8,128)}, f32[96,64,64]{2,1,0:T(8,128)})) %all-reduce.55.cloned.1.call-update) | async-done | bytes 3145744 | tf_op jit(solution)/shard_map/psum | solution.py:85
  1519.3 133.6 %convolution_add_fusion.3 = f32[3072,64]{1,0:T(8,128)} fusion(f32[3072,64]{1,0:T(8,128)S(1)} %bitcast.371, f32[3072,6144]{0,1:T(8,128)} %fusion.86, f32[6144,64]{0,1:T(8,128)S(1)} %copy-done.12), kind=kOutput, calls=%fused_computation.204 | convolution fusion | flops 14495711232 | bytes 78643200 | tf_op jit(solution)/shard_map/dot_general | solution.py:11
  1653.0 145.8 %while.137 = (s32[]{:T(128)}, f32[64,64]{1,0:T(8,128)S(1)}, f32[64]{0:T(128)S(1)}, f32[64,64]{0,1:T(8,128)S(1)}, s32[]{:T(128)}, /*index=5*/s32[]{:T(128)}) while((s32[]{:T(128)}, f32[64,64]{1,0:T(8,128)S(1)}, f32[64]{0:T(128)S(1)}, f32[64,64]{0,1:T(8,128)S(1)}, s32[]{:T(128)}, /*index=5*/s32[]{:T(128)}) %tuple.347), condition=%wide.region_13.16_spmd.clone.clone, body=%wide.region_12.15_spmd.clone.clone.sunk | while | flops 61828 | bytes 69363 | solution.py:32
  1803.0 10.4 psum.346
  1824.8 37.7 all-reduce.25.cloned.1.call-done
  1862.5 79.8 %fusion.80 = f32[3072,6144]{0,1:T(8,128)} fusion(f32[3072,6144]{0,1:T(8,128)} %fusion.86, s32[3072]{0:T(1024)S(1)} %add.526, s32[6144]{0:T(1024)S(1)} %add.532, f32[6144,64]{0,1:T(8,128)S(1)} %copy-done.13, f32[6144,64]{0,1:T(8,128)} %all-reduce.25.cloned.1.call-done, f32[3072,64]{0,1:T(8,128)S(1)} %fusion.87, f32[3072,64]{0,1:T(8,128)S(1)} %get-tuple-element.850), kind=kOutput, calls=%fused_computation.194 | convolution fusion | flops 29105455104 | bytes 155750400 | tf_op jit(solution)/shard_map/dot_general | solution.py:19
  1944.4 28.6 all-reduce.27.cloned.1.call-done
  1974.2 1189.9 %while.138 = (s32[]{:T(128)}, f32[3072,64]{0,1:T(8,128)S(1)}, f32[3072,64]{0,1:T(8,128)S(1)}, f32[64]{0:T(128)S(1)}, s32[48]{0:T(128)S(1)}, /*index=5*/s32[]{:T(128)}, f32[]{:T(128)}, s32[]{:T(128)}) while((s32[]{:T(128)}, f32[3072,64]{0,1:T(8,128)S(1)}, f32[3072,64]{0,1:T(8,128)S(1)}, f32[64]{0:T(128)S(1)}, ...), condition=%wide.region_22.25_spmd.clone.clone, body=%wide.region_17.24_spmd.clone.clone.sunk | while | flops 3416523 | bytes 4199006 | solution.py:61
  3164.7 64.1 fusion.141
  3239.2 11.9 psum.353
  3251.2 76.3 %all-reduce.53.cloned.1.call-done = (f32[6144,64]{0,1:T(8,128)}, f32[96,64,64]{2,1,0:T(8,128)}) async-done(((f32[6144,64]{0,1:T(8,128)}, f32[96,64,64]{2,1,0:T(8,128)}), (f32[6144,64]{0,1:T(8,128)}, f32[96,64,64]{2,1,0:T(8,128)})) %all-reduce.53.cloned.1.call-update) | async-done | bytes 3145744 | tf_op jit(solution)/shard_map/psum | solution.py:85
  3333.0 124.1 %convolution_add_fusion.2 = f32[3072,64]{1,0:T(8,128)} fusion(f32[3072,64]{1,0:T(8,128)S(1)} %bitcast.372, f32[3072,6144]{0,1:T(8,128)} %fusion.80, f32[6144,64]{0,1:T(8,128)S(1)} %copy-done.14), kind=kOutput, calls=%fused_computation.203 | convolution fusion | flops 14495711232 | bytes 78643200 | tf_op jit(solution)/shard_map/dot_general | solution.py:11
  3457.1 137.1 %while.139 = (s32[]{:T(128)}, f32[64,64]{1,0:T(8,128)S(1)}, f32[64]{0:T(128)S(1)}, f32[64,64]{0,1:T(8,128)S(1)}, s32[]{:T(128)}, /*index=5*/s32[]{:T(128)}) while((s32[]{:T(128)}, f32[64,64]{1,0:T(8,128)S(1)}, f32[64]{0:T(128)S(1)}, f32[64,64]{0,1:T(8,128)S(1)}, s32[]{:T(128)}, /*index=5*/s32[]{:T(128)}) %tuple.353), condition=%wide.region_29.32_spmd.clone.clone, body=%wide.region_28.31_spmd.clone.clone.sunk | while | flops 61828 | bytes 69363 | solution.py:32
  3598.4 10.4 psum.354
  3620.2 37.7 all-reduce.29.cloned.1.call-done
  3657.8 79.8 %fusion.81 = f32[3072,6144]{0,1:T(8,128)} fusion(f32[3072,6144]{0,1:T(8,128)} %fusion.80, s32[3072]{0:T(1024)S(1)} %add.526, s32[6144]{0:T(1024)S(1)} %add.532, f32[6144,64]{0,1:T(8,128)S(1)} %copy-done.15, f32[6144,64]{0,1:T(8,128)} %all-reduce.29.cloned.1.call-done, f32[3072,64]{0,1:T(8,128)S(1)} %fusion.88, f32[3072,64]{0,1:T(8,128)S(1)} %get-tuple-element.853), kind=kOutput, calls=%fused_computation.195 | convolution fusion | flops 29105455104 | bytes 155750400 | tf_op jit(solution)/shard_map/dot_general | solution.py:19
  3739.8 28.6 all-reduce.31.cloned.1.call-done
  3769.6 1191.2 %while.140 = (s32[]{:T(128)}, f32[3072,64]{0,1:T(8,128)S(1)}, f32[3072,64]{0,1:T(8,128)S(1)}, f32[64]{0:T(128)S(1)}, s32[48]{0:T(128)S(1)}, /*index=5*/s32[]{:T(128)}, f32[]{:T(128)}, s32[]{:T(128)}) while((s32[]{:T(128)}, f32[3072,64]{0,1:T(8,128)S(1)}, f32[3072,64]{0,1:T(8,128)S(1)}, f32[64]{0:T(128)S(1)}, ...), condition=%wide.region_38.41_spmd.clone.clone, body=%wide.region_33.40_spmd.clone.clone.sunk | while | flops 3416523 | bytes 4199006 | solution.py:61
  4961.2 64.0 fusion.145
  5035.8 11.9 psum.361
  5047.7 76.2 %all-reduce.51.cloned.1.call-done = (f32[6144,64]{0,1:T(8,128)}, f32[96,64,64]{2,1,0:T(8,128)}) async-done(((f32[6144,64]{0,1:T(8,128)}, f32[96,64,64]{2,1,0:T(8,128)}), (f32[6144,64]{0,1:T(8,128)}, f32[96,64,64]{2,1,0:T(8,128)})) %all-reduce.51.cloned.1.call-update) | async-done | bytes 3145744 | tf_op jit(solution)/shard_map/psum | solution.py:85
  5129.4 124.1 %convolution_add_fusion.1 = f32[3072,64]{1,0:T(8,128)} fusion(f32[3072,64]{1,0:T(8,128)S(1)} %bitcast.373, f32[3072,6144]{0,1:T(8,128)} %fusion.81, f32[6144,64]{0,1:T(8,128)S(1)} %copy-done.16), kind=kOutput, calls=%fused_computation.202 | convolution fusion | flops 14495711232 | bytes 78643200 | tf_op jit(solution)/shard_map/dot_general | solution.py:11
  5253.6 145.8 %while.141 = (s32[]{:T(128)}, f32[64,64]{1,0:T(8,128)S(1)}, f32[64]{0:T(128)S(1)}, f32[64,64]{0,1:T(8,128)S(1)}, s32[]{:T(128)}, /*index=5*/s32[]{:T(128)}) while((s32[]{:T(128)}, f32[64,64]{1,0:T(8,128)S(1)}, f32[64]{0:T(128)S(1)}, f32[64,64]{0,1:T(8,128)S(1)}, s32[]{:T(128)}, /*index=5*/s32[]{:T(128)}) %tuple.359), condition=%wide.region_45.48_spmd.clone.clone, body=%wide.region_44.47_spmd.clone.clone.sunk | while | flops 61828 | bytes 69363 | solution.py:32
  5403.5 10.4 psum.362
  5427.3 37.7 all-reduce.33.cloned.1.call-done
  5465.0 80.0 %fusion.82 = f32[3072,6144]{0,1:T(8,128)} fusion(f32[3072,6144]{0,1:T(8,128)} %fusion.81, s32[3072]{0:T(1024)S(1)} %add.526, s32[6144]{0:T(1024)S(1)} %add.532, f32[6144,64]{0,1:T(8,128)} %get-tuple-element.1289, f32[6144,64]{0,1:T(8,128)} %all-reduce.33.cloned.1.call-done, f32[3072,64]{0,1:T(8,128)S(1)} %copy-done.11, f32[3072,64]{0,1:T(8,128)S(1)} %get-tuple-element.856), kind=kOutput, calls=%fused_computation.196 | convolution fusion | flops 29105455104 | bytes 155750400 | tf_op jit(solution)/shard_map/dot_general | solution.py:19
  5549.5 26.3 all-reduce.35.cloned.1.call-done
  5577.0 1191.5 %while.142 = (s32[]{:T(128)}, f32[3072,64]{0,1:T(8,128)S(1)}, f32[3072,64]{0,1:T(8,128)S(1)}, f32[64]{0:T(128)S(1)}, s32[48]{0:T(128)S(1)}, /*index=5*/s32[]{:T(128)}, f32[]{:T(128)}, s32[]{:T(128)}) while((s32[]{:T(128)}, f32[3072,64]{0,1:T(8,128)S(1)}, f32[3072,64]{0,1:T(8,128)S(1)}, f32[64]{0:T(128)S(1)}, ...), condition=%wide.region_54.57_spmd.clone.clone, body=%wide.region_49.56_spmd.clone.clone.sunk | while | flops 3416523 | bytes 4199006 | solution.py:61
  6770.1 64.1 fusion.149
  6853.1 11.9 psum.369
  6865.1 69.3 all-reduce.49.cloned.1.call-done
  6939.9 123.9 %convolution_add_fusion = f32[3072,64]{1,0:T(8,128)} fusion(f32[3072,64]{1,0:T(8,128)S(1)} %bitcast.370, f32[3072,6144]{0,1:T(8,128)} %fusion.82, f32[6144,64]{0,1:T(8,128)S(1)} %copy-done.22), kind=kOutput, calls=%fused_computation.201 | convolution fusion | flops 14495711232 | bytes 78643200 | tf_op jit(solution)/shard_map/dot_general | solution.py:11
  7063.9 137.1 %while.143 = (s32[]{:T(128)}, f32[64,64]{1,0:T(8,128)S(1)}, f32[64]{0:T(128)S(1)}, f32[64,64]{0,1:T(8,128)S(1)}, s32[]{:T(128)}, /*index=5*/s32[]{:T(128)}) while((s32[]{:T(128)}, f32[64,64]{1,0:T(8,128)S(1)}, f32[64]{0:T(128)S(1)}, f32[64,64]{0,1:T(8,128)S(1)}, s32[]{:T(128)}, /*index=5*/s32[]{:T(128)}) %tuple.365), condition=%wide.region_61.64_spmd.clone.clone, body=%wide.region_60.63_spmd.clone.clone.sunk | while | flops 61828 | bytes 69363 | solution.py:32
  7207.7 27.0 all-reduce.47.cloned.1.call-done
  7252.1 34.1 all-reduce.37.cloned.1.call-done
  7286.3 92.8 %fusion.85 = f32[3072,6144]{0,1:T(8,128)} fusion(f32[3072,6144]{0,1:T(8,128)} %fusion.82, s32[3072]{0:T(1024)S(1)} %add.526, s32[6144]{0:T(1024)S(1)} %add.532, pred[3072]{0:T(1024)(128)(4,1)S(1)} %copy-done.29, pred[6144]{0:T(1024)(128)(4,1)S(1)} %broadcast_compare_fusion, f32[6144,64]{0,1:T(8,128)} %get-tuple-element.1287, ...), kind=kOutput, calls=%fused_computation.199 | convolution fusion | flops 29180952576 | bytes 155759616 | tf_op jit(solution)/shard_map/dot_general | solution.py:19
  7379.0 73.0 copy.64
  (5328 shorter events, 4589.8 us)
Async XLA Ops:
  7.2 156.6 %all-reduce.23.cloned.1.call-start = ((), (), s32[]{:S(2)}) async-start(), calls=%async_computation | async-start | bytes 1572864 | tf_op jit(solution)/shard_map/psum | solution.py:103
  132.2 1381.7 %all-reduce.55.cloned.1.call-start = ((), (), s32[]{:S(2)}) async-start(), calls=%async_computation.16 | async-start | bytes 9437184 | tf_op jit(solution)/shard_map/psum | solution.py:85
  1350.2 64.6 copy-start.4
  1350.3 512.2 %copy-start = (f32[3072,64]{0,1:T(8,128)}, f32[3072,64]{0,1:T(8,128)S(1)}, u32[]{:S(2)}) copy-start(f32[3072,64]{0,1:T(8,128)S(1)} %get-tuple-element.850) | copy-start | bytes 2359300
  1424.5 374.4 %all-reduce.39.cloned.1.call-start = ((), (), s32[]{:S(2)}) async-start(), calls=%async_computation.8 | async-start | bytes 3145728 | tf_op jit(solution)/shard_map/psum | solution.py:111
  1513.9 5.4 copy-start.12
  1653.0 209.5 %all-reduce.25.cloned.1.call-start = ((), (), s32[]{:S(2)}) async-start(), calls=%async_computation.1 | async-start | bytes 3145728 | tf_op jit(solution)/shard_map/psum | solution.py:85
  1798.9 14.5 copy-start.17
  1821.3 41.1 copy-start.13
  1824.7 148.3 %all-reduce.27.cloned.1.call-start = ((), (), s32[]{:S(2)}) async-start(), calls=%async_computation.2 | async-start | bytes 1572864 | tf_op jit(solution)/shard_map/psum | solution.py:103
  1944.3 1383.2 %all-reduce.53.cloned.1.call-start = ((), (), s32[]{:S(2)}) async-start(), calls=%async_computation.15 | async-start | bytes 9437184 | tf_op jit(solution)/shard_map/psum | solution.py:85
  3164.2 64.6 copy-start.6
  3164.2 493.6 %copy-start.2 = (f32[3072,64]{0,1:T(8,128)}, f32[3072,64]{0,1:T(8,128)S(1)}, u32[]{:S(2)}) copy-start(f32[3072,64]{0,1:T(8,128)S(1)} %get-tuple-element.853) | copy-start | bytes 2359300
  3238.4 355.9 %all-reduce.41.cloned.1.call-start = ((), (), s32[]{:S(2)}) async-start(), calls=%async_computation.9 | async-start | bytes 3145728 | tf_op jit(solution)/shard_map/psum | solution.py:111
  3327.5 5.4 copy-start.14
  3457.1 200.7 %all-reduce.29.cloned.1.call-start = ((), (), s32[]{:S(2)}) async-start(), calls=%async_computation.3 | async-start | bytes 3145728 | tf_op jit(solution)/shard_map/psum | solution.py:85
  3594.3 14.5 copy-start.19
  3616.7 41.1 copy-start.15
  3620.1 148.3 %copy-start.28 = (pred[3072]{0:T(1024)(128)(4,1)S(1)}, pred[3072]{0:T(1024)(128)(4,1)}, u32[]{:S(2)}) copy-start(pred[3072]{0:T(1024)(128)(4,1)} %get-tuple-element.1344) | copy-start | bytes 9220
  3620.1 148.3 %all-reduce.31.cloned.1.call-start = ((), (), s32[]{:S(2)}) async-start(), calls=%async_computation.4 | async-start | bytes 1572864 | tf_op jit(solution)/shard_map/psum | solution.py:103
  3739.7 1384.3 %all-reduce.51.cloned.1.call-start = ((), (), s32[]{:S(2)}) async-start(), calls=%async_computation.14 | async-start | bytes 9437184 | tf_op jit(solution)/shard_map/psum | solution.py:85
  5034.9 364.5 %all-reduce.43.cloned.1.call-start = ((), (), s32[]{:S(2)}) async-start(), calls=%async_computation.10 | async-start | bytes 3145728 | tf_op jit(solution)/shard_map/psum | solution.py:111
  5124.0 5.4 copy-start.16
  5253.6 211.5 %all-reduce.33.cloned.1.call-start = ((), (), s32[]{:S(2)}) async-start(), calls=%async_computation.5 | async-start | bytes 3145728 | tf_op jit(solution)/shard_map/psum | solution.py:85
  5423.9 41.1 copy-start.11
  5427.3 119.9 %copy-start.5 = (f32[3072,64]{0,1:T(8,128)S(1)}, f32[3072,64]{0,1:T(8,128)}, u32[]{:S(2)}) copy-start(f32[3072,64]{0,1:T(8,128)} %copy-done.4) | copy-start | bytes 2359300
  5427.3 148.5 %all-reduce.35.cloned.1.call-start = ((), (), s32[]{:S(2)}) async-start(), calls=%async_computation.6 | async-start | bytes 1572864 | tf_op jit(solution)/shard_map/psum | solution.py:103
  5545.0 30.8 copy-start.27
  5547.1 1387.3 %all-reduce.49.cloned.1.call-start = ((), (), s32[]{:S(2)}) async-start(), calls=%async_computation.13 | async-start | bytes 9437184 | tf_op jit(solution)/shard_map/psum | solution.py:85
  6768.5 65.7 copy-start.8
  6845.2 1.1 copy-start.7
  6845.2 357.7 %all-reduce.45.cloned.1.call-start = ((), (), s32[]{:S(2)}) async-start(), calls=%async_computation.11 | async-start | bytes 3145728 | tf_op jit(solution)/shard_map/psum | solution.py:111
  6845.3 7.1 copy-start.9
  6938.1 1.9 copy-start.22
  7063.8 137.8 %copy-start.21 = (f32[3072,64]{0,1:T(8,128)S(1)}, f32[3072,64]{0,1:T(8,128)}, u32[]{:S(2)}) copy-start(f32[3072,64]{0,1:T(8,128)} %all-reduce.35.cloned.1.call-done) | copy-start | bytes 2359300
  7063.8 142.4 %copy-start.10 = (f32[3072,64]{0,1:T(8,128)S(1)}, f32[3072,64]{0,1:T(8,128)}, u32[]{:S(2)}) copy-start(f32[3072,64]{0,1:T(8,128)} %copy-done.8) | copy-start | bytes 2359300
  7063.9 170.8 %all-reduce.47.cloned.1.call-start = ((), (), s32[]{:S(2)}) async-start(), calls=%async_computation.12 | async-start | bytes 327680 | tf_op jit(solution)/shard_map/psum | solution.py:114
  7207.6 78.6 %all-reduce.37.cloned.1.call-start = ((), (), s32[]{:S(2)}) async-start(), calls=%async_computation.7 | async-start | bytes 3145728 | tf_op jit(solution)/shard_map/psum | solution.py:85
  7245.4 3.4 copy-start.18
  7245.4 3.4 copy-start.20
  7245.4 4.1 copy-start.1
  7245.4 4.1 copy-start.3
  7249.5 1.9 copy-start.23
  7249.5 1.9 copy-start.24
  7249.5 1.9 copy-start.25
  7249.6 1.9 copy-start.26
  7249.6 36.7 copy-start.29
Sparse Core Ops, SparseCore 0:
  132.3 31.3 all-reduce.22
  1424.6 89.2 all-reduce.54
  1653.1 45.9 all-reduce.38
  1824.8 37.5 all-reduce.24
  1944.4 28.5 all-reduce.26
  3238.5 88.9 all-reduce.52
  3457.2 45.8 all-reduce.40
  3620.2 37.5 all-reduce.28
  3739.8 28.5 all-reduce.30
  5035.1 88.8 all-reduce.50
  5253.7 45.9 all-reduce.42
  5427.4 37.5 all-reduce.32
  5547.2 28.5 all-reduce.34
  6845.3 89.0 all-reduce.48
  7064.0 45.8 all-reduce.44
  7207.7 26.9 all-reduce.46
  7248.9 37.2 all-reduce.36
where the time goes:
time: 7500 us; the launch traced here: 7460 us
  blocking collectives  3130 us (42%)
  matrix products  1520 us (20%)
  loops' own time  866 us (12%)
  other arithmetic  791 us (11%)
  waiting for transfers between devices  587 us (8%)
  local copies, waits for them, and re-layouts  551 us (7%)
    psum x256, blocking collectives, qr_column(): stats = lax.psum(jnp.stack([head, jnp.sum(below * below)]), 'row')  1570 us
    psum x256, blocking collectives, qr_column(): lax.psum(jnp.dot(house, work, precision=PREC_HIGH, preferred_element_type...  1490 us
    another operation x4, loops' own time, panel_qr(): return lax.fori_loop(0, block, qr_column, begin)  693 us
    dot_general x20, matrix products, mat_dot(): jnp.dot(left, right, precision=PREC_HIGH, preferred_element_type=jnp.floa...  532 us
    psum x8, waiting for transfers between devices, rows_to_cols(): return lax.psum(picked.reshape(cols_loc, block), 'row')  446 us
    another operation x256, other arithmetic, qr_column(): stats = lax.psum(jnp.stack([head, jnp.sum(below * below)]), 'row')  347 us
    dot_general x4, matrix products, dot_nt(): lax.dot_general(left, right, (((1,), (1,)), ((), ())), precision=PREC_HIG...  332 us
    reshape x4, matrix products, cols_to_rows(): x_cols.reshape(col_blocks, block, block)  256 us

commit v1 on v0

v1 whole, which is shorter than its diff:
```python
import functools

import jax
import jax.numpy as jnp
from jax import lax
from jax.experimental import pallas as pl
from jax.experimental.pallas import tpu as pltpu
from jax.sharding import PartitionSpec as P

PANELS = 4
NB = 64
NB3 = 3 * NB
LANES = 128
N = 12288
HALF = N // 2
ROWS = N // 4
F32 = jnp.float32
BF16 = jnp.bfloat16
CH = 2048
NCH = N // CH
TR, TC = 512, 1024
NT = ROWS // TR
VMEM_LIMIT = 62 * 1024 * 1024


def lane_of_block(blk):
    pos = (blk % 2) * HALF + (blk // 2) * NB
    return pos // LANES, pos % LANES


def span(start, size):
    return pl.ds(pl.multiple_of(start, size), size)


def split3(x):
    x1 = x.astype(BF16)
    r = x - x1.astype(F32)
    x2 = r.astype(BF16)
    x3 = (r - x2.astype(F32)).astype(BF16)
    return x1, x2, x3


def dot_nn(a, b):
    return lax.dot_general(a, b, (((1,), (0,)), ((), ())), preferred_element_type=F32)


def dot_nt(a, b):
    return lax.dot_general(a, b, (((1,), (1,)), ((), ())), preferred_element_type=F32)


def hi_nn(a, b):
    return lax.dot_general(a, b, (((1,), (0,)), ((), ())), precision=lax.Precision.HIGHEST, preferred_element_type=F32)


def hi_tn(a, b):
    return lax.dot_general(a, b, (((0,), (0,)), ((), ())), precision=lax.Precision.HIGHEST, preferred_element_type=F32)


def stack3(x):
    return jnp.concatenate(split3(x), axis=0)


def fold9(acc):
    r = acc[0:NB] + (acc[NB:LANES] + acc[LANES:NB3])
    return r[:, 0:NB] + (r[:, NB:LANES] + r[:, LANES:NB3])


def small_by_wide(c_stack, b):
    b1, b2, b3 = split3(b)
    r1 = dot_nn(c_stack, b1)
    r2 = dot_nn(c_stack[0:LANES], b2)
    r3 = dot_nn(c_stack[0:NB], b3)
    return r1[0:NB] + ((r1[NB:LANES] + r2[0:NB]) + (r1[LANES:NB3] + (r2[NB:LANES] + r3)))


def iota2(shape, dim):
    return lax.broadcasted_iota(jnp.int32, shape, dim)


def params(**kw):
    return pltpu.CompilerParams(vmem_limit_bytes=VMEM_LIMIT, **kw)


def interleave_kernel(a_ref, b_ref, o_ref):
    lo = iota2((NB, LANES), 1) < NB
    for m in range(12):
        a = a_ref[0, :, m * LANES:(m + 1) * LANES]
        b = b_ref[0, :, m * LANES:(m + 1) * LANES]
        o_ref[0, :, (2 * m) * LANES:(2 * m + 1) * LANES] = jnp.where(lo, a, pltpu.roll(b, NB, 1))
        o_ref[0, :, (2 * m + 1) * LANES:(2 * m + 2) * LANES] = jnp.where(lo, pltpu.roll(a, NB, 1), b)


def interleave(gathered):
    width = 12 * LANES
    return pl.pallas_call(
        interleave_kernel,
        grid=(2, 2, 2),
        in_specs=[
            pl.BlockSpec((1, NB, width), lambda q, c, m: (q * 4 + c, 0, m)),
            pl.BlockSpec((1, NB, width), lambda q, c, m: (q * 4 + c + 2, 0, m)),
        ],
        out_specs=pl.BlockSpec((1, NB, 2 * width), lambda q, c, m: (q, 0, c * 2 + m)),
        out_shape=jax.ShapeDtypeStruct((2, NB, N), F32),
        compiler_params=params(),
        name="interleave",
    )(gathered, gathered)


def qr_kernel(k, p_ref, vt_ref, vts_ref, band_ref, t_ref, xb_ref, rt_ref, inv_ref, tau_ref, gram_ref):
    piv_tile, piv_off = lane_of_block(k + 1)
    diag_tile, diag_off = lane_of_block(k)
    piv = slice(piv_tile * LANES, piv_tile * LANES + LANES)

    def copy_in(c, _):
        at = span(c * CH, CH)
        vt_ref[:, at] = p_ref[:, at]
        return 0

    lax.fori_loop(0, NCH, copy_in, 0)
    lane64 = iota2((NB, LANES), 1)
    row64 = iota2((NB, LANES), 0)
    for cls in range(2):
        sl = slice(cls * HALF, cls * HALF + LANES)
        blk = 2 * (lane64 // NB) + cls
        vt_ref[:, sl] = jnp.where(blk >= k + 1, p_ref[:, sl], 0.0)
    rt_ref[...] = jnp.zeros_like(rt_ref)
    inv_ref[...] = jnp.zeros_like(inv_ref)
    tau_ref[...] = jnp.zeros_like(tau_ref)

    for g0 in range(8):
        r0 = 8 * g0
        groups = 8 - g0
        height = 8 * groups
        lane = iota2((height, LANES), 1)
        row_b = r0 + iota2((height, LANES), 0)
        row1 = r0 + iota2((height, 1), 0)

        def step(jj, _, r0=r0, groups=groups, height=height, lane=lane, row_b=row_b, row1=row1):
            j = r0 + jj
            at_piv = lane == piv_off + j

            def dots(c, accs):
                at = span(c * CH, CH)
                xb = jnp.broadcast_to(vt_ref[pl.ds(j, 1), at], (8, CH))
                xb_ref[:, at] = xb
                out = []
                for g in range(groups):
                    prod = vt_ref[r0 + 8 * g:r0 + 8 * g + 8, at] * xb
                    parts = [prod[:, t * LANES:(t + 1) * LANES] for t in range(CH // LANES)]
                    while len(parts) > 1:
                        parts = [parts[i] + parts[i + 1] for i in range(0, len(parts), 2)]
                    out.append(accs[g] + parts[0])
                return tuple(out)

            accs = lax.fori_loop(0, NCH, dots, tuple(jnp.zeros((8, LANES), F32) for _ in range(groups)))
            d = jnp.sum(jnp.concatenate(accs, axis=0), axis=1, keepdims=True)
            pv = jnp.sum(jnp.where(at_piv, vt_ref[r0:NB, piv], 0.0), axis=1, keepdims=True)
            is_j = row1 == j
            nrm2 = jnp.sum(jnp.where(is_j, d, 0.0), axis=0, keepdims=True)
            alpha = jnp.sum(jnp.where(is_j, pv, 0.0), axis=0, keepdims=True)
            norm = jnp.sqrt(nrm2)
            beta = jnp.where(alpha >= 0.0, -norm, norm)
            tau = (beta - alpha) / beta
            inv = 1.0 / (alpha - beta)
            proj = inv * (d - beta * pv)
            s = jnp.where(row1 > j, tau * proj * inv, 0.0)
            xb_ref[:, piv] = xb_ref[:, piv] - jnp.where(lane[0:8] == piv_off + j, beta, 0.0)
            sb = jnp.broadcast_to(s, (height, LANES))

            def update(c, _):
                at = span(c * CH, CH)
                xb = xb_ref[:, at]
                for g in range(groups):
                    sg = sb[8 * g:8 * g + 8]
                    blk = vt_ref[r0 + 8 * g:r0 + 8 * g + 8, at]
                    vt_ref[r0 + 8 * g:r0 + 8 * g + 8, at] = jnp.concatenate(
                        [blk[:, t * LANES:(t + 1) * LANES] - sg * xb[:, t * LANES:(t + 1) * LANES] for t in range(CH // LANES)], axis=1)
                return 0

            lax.fori_loop(0, NCH, update, 0)
            r_col = jnp.where(is_j, beta, jnp.where(row1 > j, pv - s * (alpha - beta), 0.0))
            rt_ref[r0:NB] = jnp.where(lane == j, r_col, rt_ref[r0:NB])
            vt_ref[r0:NB, piv] = jnp.where(at_piv & (row_b > j), 0.0, vt_ref[r0:NB, piv])
            inv_ref[r0:NB] = jnp.where(row_b == j, inv, inv_ref[r0:NB])
            tau_ref[r0:NB] = jnp.where(row_b == j, tau, tau_ref[r0:NB])
            return 0

        lax.fori_loop(0, 8, step, 0)

    vt_ref[:, piv] = jnp.where(lane64 == piv_off + row64, 0.0, vt_ref[:, piv])
    inv_b = inv_ref[...]
    gram_ref[...] = jnp.zeros_like(gram_ref)

    def finish(c, _):
        at = span(c * CH, CH)
        blk = vt_ref[:, at]
        blk = jnp.concatenate([blk[:, t * LANES:(t + 1) * LANES] * inv_b for t in range(CH // LANES)], axis=1)
        lanes = c * CH + iota2((NB, CH), 1)
        blk = jnp.where(lanes == piv_tile * LANES + piv_off + iota2((NB, CH), 0), 1.0, blk)
        vt_ref[:, at] = blk
        st = stack3(blk)
        vts_ref[:, at] = st
        gram_ref[...] += dot_nt(st, st)
        return 0

    lax.fori_loop(0, NCH, finish, 0)
    gram = fold9(gram_ref[...])
    rr = iota2((NB, NB), 0)
    cc = iota2((NB, NB), 1)
    t_mat = jnp.where(rr == cc, tau_ref[:, 0:NB], 0.0)
    size = 1
    while size < NB:
        pair = (rr // (2 * size) == cc // (2 * size)) & ((rr // size) % 2 == 0) & ((cc // size) % 2 == 1)
        t_mat = t_mat - hi_nn(t_mat, hi_nn(jnp.where(pair, gram, 0.0), t_mat))
        size *= 2
    t_ref[...] = t_mat
    diag = p_ref[:, diag_tile * LANES:diag_tile * LANES + LANES].T[diag_off:diag_off + NB]
    band_ref[0:NB] = jnp.where(rr >= cc, diag, 0.0)
    band_ref[NB:LANES] = rt_ref[...].T[0:NB]


def panel_qr(k, panel):
    return pl.pallas_call(
        functools.partial(qr_kernel, k),
        out_shape=(
            jax.ShapeDtypeStruct((NB, N), F32),
            jax.ShapeDtypeStruct((NB3, N), BF16),
            jax.ShapeDtypeStruct((LANES, NB), F32),
            jax.ShapeDtypeStruct((NB, NB), F32),
        ),
        scratch_shapes=[
            pltpu.VMEM((8, N), F32),
            pltpu.VMEM((NB, LANES), F32),
            pltpu.VMEM((NB, LANES), F32),
            pltpu.VMEM((NB, LANES), F32),
            pltpu.VMEM((NB3, NB3), F32),
        ],
        compiler_params=params(),
        name=f"panel_qr{k}",
    )(panel)


LOWER_TILES = [(i, j) for i in range(NT) for j in range(i + 1)]


def global_ids(pq_ref, tile_i, tile_j, shape):
    rloc = tile_i * TR + iota2(shape, 0)
    cloc = tile_j * TC + iota2(shape, 1)
    row = ((rloc >> 6) * 4 + pq_ref[0]) * NB + (rloc & 63)
    col = ((cloc >> 6) * 2 + pq_ref[1]) * NB + (cloc & 63)
    return row, col


def av_kernel(ti_ref, tj_ref, pq_ref, l_ref, vtc_ref, vtp_ref, z_ref, vrt_ref, vr_ref, ls_ref, vtr_ref, acc1_ref, acc2_ref):
    step = pl.program_id(0)
    ti = ti_ref[step]
    tj = tj_ref[step]
    proc_row = pq_ref[0]
    proc_col = pq_ref[1]
    upper = (proc_row >> 1) == 1

    @pl.when(step == 0)
    def _():
        acc1_ref[...] = jnp.zeros_like(acc1_ref)
        acc2_ref[...] = jnp.zeros_like(acc2_ref)

        def pick(i, _):
            tile = vtp_ref[:, span(i * LANES, LANES)].T
            vr_ref[span(i * NB, NB), :] = jnp.where(upper, tile[NB:LANES], tile[0:NB])
            return 0

        lax.fori_loop(0, 48, pick, 0)

        def back(m, _):
            tile = vr_ref[span(m * LANES, LANES), :].T
            vrt_ref[:, span(m * LANES, LANES)] = tile
            vtr_ref[:, span(m * LANES, LANES)] = stack3(tile)
            return 0

        lax.fori_loop(0, 24, back, 0)

    def put(tile):
        s1, s2, s3 = split3(tile)
        ls_ref[0] = s1
        ls_ref[1] = s2
        ls_ref[2] = s3

    @pl.when(ti == tj)
    def _():
        row, col = global_ids(pq_ref, ti, tj, (TR, TC))
        put(jnp.where(row == col, 0.5, 1.0) * l_ref[...])

    @pl.when(ti != tj)
    def _():
        put(l_ref[...])

    cols = span(tj * TC, TC)
    rows = span(ti * TR, TR)
    vc = vtc_ref[:, cols]
    acc1_ref[rows, :] += dot_nt(ls_ref[0], vc) + (dot_nt(ls_ref[1], vc) + dot_nt(ls_ref[2], vc))
    vr = vtr_ref[:, rows]
    acc2_ref[:, cols] += dot_nn(vr, ls_ref[0]) + (dot_nn(vr, ls_ref[1]) + dot_nn(vr, ls_ref[2]))

    @pl.when(step == len(LOWER_TILES) - 1)
    def _():
        def out(i, _):
            at = span(i * LANES, LANES)
            blk = acc1_ref[span(i * NB, NB), :]
            blk = blk[:, 0:NB] + (blk[:, NB:LANES] + blk[:, LANES:NB3])
            wide = jnp.concatenate([jnp.where(upper, 0.0, blk), jnp.where(upper, blk, 0.0)], axis=0).T
            own = acc2_ref[0:NB, at] + (acc2_ref[NB:LANES, at] + acc2_ref[LANES:NB3, at])
            for cls in range(2):
                z_ref[:, span(cls * HALF + i * LANES, LANES)] = (
                    jnp.where(proc_col == cls, own, 0.0) + jnp.where((proc_row & 1) == cls, wide, 0.0))
            return 0

        lax.fori_loop(0, 48, out, 0)


def times_matrix(pq, l_loc, vt, vts):
    tile_i = jnp.array([t[0] for t in LOWER_TILES], jnp.int32)
    tile_j = jnp.array([t[1] for t in LOWER_TILES], jnp.int32)
    return pl.pallas_call(
        av_kernel,
        grid_spec=pltpu.PrefetchScalarGridSpec(
            num_scalar_prefetch=3,
            grid=(len(LOWER_TILES),),
            in_specs=[
                pl.BlockSpec((TR, TC), lambda s, ti, tj, pq: (ti[s], tj[s])),
                pl.BlockSpec((NB3, HALF), lambda s, ti, tj, pq: (0, pq[1])),
                pl.BlockSpec((NB, HALF), lambda s, ti, tj, pq: (0, pq[0] & 1)),
            ],
            out_specs=[
                pl.BlockSpec((NB, N), lambda s, ti, tj, pq: (0, 0)),
                pl.BlockSpec((NB, ROWS), lambda s, ti, tj, pq: (0, 0)),
            ],
            scratch_shapes=[
                pltpu.VMEM((ROWS, NB), F32),
                pltpu.VMEM((3, TR, TC), BF16),
                pltpu.VMEM((NB3, ROWS), BF16),
                pltpu.VMEM((ROWS, NB3), F32),
                pltpu.VMEM((NB3, HALF), F32),
            ],
        ),
        out_shape=(jax.ShapeDtypeStruct((NB, N), F32), jax.ShapeDtypeStruct((NB, ROWS), F32)),
        compiler_params=params(),
        name="times_matrix",
    )(tile_i, tile_j, pq, l_loc, vts, vt)


WCH = 1024


def w_kernel(k, *refs):
    z_ref, vt_ref, vts_ref, t_ref = refs[:4]
    prev = refs[4:4 + 2 * k]
    rest = refs[4 + 2 * k:]
    last = k == PANELS - 1
    if last:
        w_ref, sacc_ref = rest[:2]
        cacc = rest[2:]
    else:
        a0_ref, w_ref, p_ref, sacc_ref = rest[:4]
        cacc = rest[4:]
    sacc_ref[...] = jnp.zeros_like(sacc_ref)
    for ref in cacc:
        ref[...] = jnp.zeros_like(ref)

    def sums(c, _):
        at = span(c * WCH, WCH)
        vs = vts_ref[:, at]
        sacc_ref[...] += dot_nt(vs, stack3(z_ref[:, at]))
        for ref, src in zip(cacc, prev):
            ref[...] += dot_nt(stack3(src[:, at]), vs)
        return 0

    lax.fori_loop(0, N // WCH, sums, 0)
    t_mat = t_ref[...]
    s_mat = fold9(sacc_ref[...])
    coef = [fold9(ref[...]) for ref in cacc]
    for j in range(k):
        c_v, c_w = coef[2 * j], coef[2 * j + 1]
        s_mat = s_mat - (hi_tn(c_v, c_w) + hi_tn(c_w, c_v))
    m_mat = hi_tn(t_mat, hi_nn(s_mat, t_mat))
    terms = [stack3(t_mat.T), stack3((-0.5 * m_mat).T)]
    for j in range(k):
        terms.append(stack3((-hi_nn(coef[2 * j + 1], t_mat)).T))
        terms.append(stack3((-hi_nn(coef[2 * j], t_mat)).T))
    srcs = [z_ref, vt_ref] + list(prev)

    def write_w(c, _):
        at = span(c * WCH, WCH)
        acc = small_by_wide(terms[0], srcs[0][:, at])
        for term, src in zip(terms[1:], srcs[1:]):
            acc = acc + small_by_wide(term, src[:, at])
        w_ref[:, at] = acc
        return 0

    lax.fori_loop(0, N // WCH, write_w, 0)
    lane64 = iota2((NB, LANES), 1)
    for cls in range(2):
        sl = slice(cls * HALF, cls * HALF + LANES)
        w_ref[:, sl] = jnp.where(2 * (lane64 // NB) + cls >= k + 1, w_ref[:, sl], 0.0)
    if last:
        return
    tile, off = lane_of_block(k + 1)
    pairs = [(prev[2 * j], prev[2 * j + 1]) for j in range(k)] + [(vt_ref, w_ref)]
    facs = []
    for v, w in pairs:
        v_rows = v[:, tile * LANES:tile * LANES + LANES].T[off:off + NB]
        w_rows = w[:, tile * LANES:tile * LANES + LANES].T[off:off + NB]
        facs.append((stack3(w_rows), v))
        facs.append((stack3(v_rows), w))

    def write_p(c, _):
        at = span(c * WCH, WCH)
        acc = small_by_wide(facs[0][0], facs[0][1][:, at])
        for fac, src in facs[1:]:
            acc = acc + small_by_wide(fac, src[:, at])
        p_ref[:, at] = a0_ref[:, at] - acc
        return 0

    lax.fori_loop(0, N // WCH, write_p, 0)


def make_w(k, z, vt, vts, t_mat, prev, a0_next):
    last = k == PANELS - 1
    outs = [jax.ShapeDtypeStruct((NB, N), F32)] * (1 if last else 2)
    args = [z, vt, vts, t_mat, *prev] + ([] if last else [a0_next])
    res = pl.pallas_call(
        functools.partial(w_kernel, k),
        out_shape=tuple(outs),
        scratch_shapes=[pltpu.VMEM((NB3, NB3), F32)] * (1 + 2 * k),
        compiler_params=params(),
        name=f"make_w{k}",
    )(*args)
    return (res[0], None) if last else res


PCH = 512


def prep_kernel(pq_ref, *refs):
    vr, wr, vc, wc = refs[0:4], refs[4:8], refs[8:12], refs[12:16]
    x_ref, y_ref = refs[16:]
    upper = (pq_ref[0] >> 1) == 1
    for pos, group in enumerate((vr, wr)):
        for pair in range(2):
            two = jnp.concatenate([group[2 * pair][...], group[2 * pair + 1][...]], axis=0).T
            half = jnp.concatenate(
                [jnp.where(upper, two[LANES * i + NB:LANES * i + LANES], two[LANES * i:LANES * i + NB]) for i in range(PCH // LANES)], axis=0)
            lanes = slice((2 * pos + pair) * LANES, (2 * pos + pair) * LANES + LANES)
            for s, part in enumerate(split3(half)):
                x_ref[s, :, lanes] = part
    for pos, group in enumerate((wc, vc)):
        for j in range(4):
            rows = slice((4 * pos + j) * NB, (4 * pos + j) * NB + NB)
            for s, part in enumerate(split3(group[j][...])):
                y_ref[s, rows, :] = part


def prep(pq, vts, wts):
    row_spec = pl.BlockSpec((NB, PCH), lambda c, pq: (0, (pq[0] & 1) * (HALF // PCH) + c))
    col_spec = pl.BlockSpec((NB, PCH), lambda c, pq: (0, pq[1] * (HALF // PCH) + c))
    return pl.pallas_call(
        prep_kernel,
        grid_spec=pltpu.PrefetchScalarGridSpec(
            num_scalar_prefetch=1,
            grid=(HALF // PCH,),
            in_specs=[row_spec] * 8 + [col_spec] * 8,
            out_specs=[
                pl.BlockSpec((3, PCH // 2, 512), lambda c, pq: (0, c, 0)),
                pl.BlockSpec((3, 512, PCH), lambda c, pq: (0, 0, c)),
            ],
        ),
        out_shape=(jax.ShapeDtypeStruct((3, ROWS, 512), BF16), jax.ShapeDtypeStruct((3, 512, HALF), BF16)),
        compiler_params=params(),
        name="prep",
    )(pq, *vts, *wts, *vts, *wts)


def final_kernel(pq_ref, l_ref, x_ref, y_ref, o_ref):
    ti = pl.program_id(0)
    tj = pl.program_id(1)

    @pl.when(tj > ti)
    def _():
        o_ref[...] = jnp.zeros_like(o_ref)

    @pl.when(tj <= ti)
    def _():
        x1, x2, x3 = x_ref[0], x_ref[1], x_ref[2]
        width = 256
        for c in range(TC // width):
            cols = slice(c * width, (c + 1) * width)
            y1, y2, y3 = y_ref[0, :, cols], y_ref[1, :, cols], y_ref[2, :, cols]
            upd = dot_nn(x3, y1) + dot_nn(x1, y3) + dot_nn(x2, y2) + dot_nn(x2, y1) + dot_nn(x1, y2) + dot_nn(x1, y1)
            rloc = ti * TR + iota2((TR, width), 0)
            cloc = tj * TC + c * width + iota2((TR, width), 1)
            row = ((rloc >> 6) * 4 + pq_ref[0]) * NB + (rloc & 63)
            col = ((cloc >> 6) * 2 + pq_ref[1]) * NB + (cloc & 63)
            keep = (row >= col) & (col >= PANELS * NB)
            o_ref[:, cols] = jnp.where(keep, l_ref[:, cols] - upd, 0.0)


def final_update(pq, l_loc, x, y):
    return pl.pallas_call(
        final_kernel,
        grid_spec=pltpu.PrefetchScalarGridSpec(
            num_scalar_prefetch=1,
            grid=(NT, NT),
            in_specs=[
                pl.BlockSpec((TR, TC), lambda i, j, pq: (i, jnp.minimum(i, j))),
                pl.BlockSpec((3, TR, 512), lambda i, j, pq: (0, i, 0)),
                pl.BlockSpec((3, 512, TC), lambda i, j, pq: (0, 0, jnp.minimum(i, j))),
            ],
            out_specs=pl.BlockSpec((TR, TC), lambda i, j, pq: (i, j)),
        ),
        out_shape=jax.ShapeDtypeStruct((ROWS, HALF), F32),
        compiler_params=params(),
        name="final_update",
    )(pq, l_loc, x, y)


def solution(mesh):
    mat_spec = P(("part", "row"), None, "col")

    def local_step(l_blk):
        l_loc = l_blk.reshape(ROWS, HALF)
        pq = jnp.stack([lax.axis_index("row"), lax.axis_index("col")]).astype(jnp.int32)
        first = l_loc[:, 0:LANES].T
        start = [interleave(lax.all_gather(first[NB * h:NB * h + NB], ("col", "row"))) for h in range(2)]
        panels0 = [start[k // 2][k % 2] for k in range(PANELS)]
        panel = panels0[0]
        prev = []
        v_list, w_list, band_list, vec_list, tri_list = [], [], [], [], []
        for k in range(PANELS):
            vt, vts, band, t_mat = panel_qr(k, panel)
            z_part, v_rows = times_matrix(pq, l_loc, vt, vts)
            z = lax.psum(z_part, ("col", "row"))
            wt, panel = make_w(k, z, vt, vts, t_mat, prev, panels0[k + 1] if k + 1 < PANELS else None)
            prev = prev + [vt, wt]
            v_list.append(vt)
            w_list.append(wt)
            band_list.append(band)
            vec_list.append(v_rows)
            tri_list.append(t_mat)
        x, y = prep(pq, v_list, w_list)
        l_out = final_update(pq, l_loc, x, y)
        return l_out.reshape(l_blk.shape), jnp.stack(band_list), jnp.stack(vec_list).transpose(0, 2, 1), jnp.stack(tri_list)

    return jax.shard_map(local_step, mesh=mesh, in_specs=(mat_spec,), out_specs=(mat_spec, P("part"), P(None, ("part", "row"), None), P("part")), check_vma=False)
```

time: 7500 us -> 1040 us (0.14)
  blocking collectives: 3130 us -> 0 us
  matrix products: 1520 us -> 0 us
  loops' own time: 866 us -> 0 us
  other arithmetic: 791 us -> 4.25 us
  Pallas kernels: 0 us -> 744 us
  local copies, waits for them, and re-layouts: 551 us -> 17.9 us
  waiting for transfers between devices: 587 us -> 253 us
    psum x519 -> x0, blocking collectives: 3130 us -> none  [the longest x256 1570 us: qr_column(): stats = lax.psum(jnp.stack([head, jnp.sum(below * below)]), 'row')]
    dot_general x548 -> x0, matrix products: 1260 us -> none  [the longest x20 532 us: mat_dot(): jnp.dot(left, right, precision=PREC_HIGH, preferred_element_type=jnp.floa...]
    another operation x8 -> x0, loops' own time: 866 us -> none  [the longest x4 693 us: panel_qr(): return lax.fori_loop(0, block, qr_column, begin)]
    pallas_call x0 -> x16, Pallas kernels: none -> 744 us  [the longest x4 285 us: times_matrix(): pl.pallas_call(av_kernel, grid_spec=pltpu.PrefetchScalarGridSpec(num_scal...]
    psum x17 -> x4, waiting for transfers between devices: 587 us -> 212 us  [local_step(): z = lax.psum(z_part, ('col', 'row'))]
    another operation x257 -> x1, other arithmetic: 349 us -> 0.59 us  [local_step(): jnp.stack([lax.axis_index('row'), lax.axis_index('col')]).astype(jnp.int32)]
    reshape x4 -> x0, matrix products: 256 us -> none  [cols_to_rows(): x_cols.reshape(col_blocks, block, block)]
    select_n x1302 -> x0, other arithmetic: 181 us -> none  [the longest x256 103 us: qr_column(): vecs = jnp.where(pick, house[:, None], vecs)]
where the time goes in v1:
time: 1040 us
  Pallas kernels  744 us (72%)
  waiting for transfers between devices  253 us (24%)
  local copies, waits for them, and re-layouts  17.9 us (2%)
  between operations  14.4 us (1%)
    pallas_call x4, Pallas kernels, times_matrix(): pl.pallas_call(av_kernel, grid_spec=pltpu.PrefetchScalarGridSpec(num_scal...  285 us
    psum x4, waiting for transfers between devices, local_step(): z = lax.psum(z_part, ('col', 'row'))  212 us
    pallas_call x4, Pallas kernels, make_w(): pl.pallas_call(functools.partial(w_kernel, k), out_shape=tuple(outs), scr...  160 us
    pallas_call x4, Pallas kernels, panel_qr(): pl.pallas_call(functools.partial(qr_kernel, k), out_shape=(jax.ShapeDtype...  150 us
    pallas_call x1, Pallas kernels, final_update(): pl.pallas_call(final_kernel, grid_spec=pltpu.PrefetchScalarGridSpec(num_s...  107 us
    all_gather x2, waiting for transfers between devices, local_step(): lax.all_gather(first[NB * h:NB * h + NB], ('col', 'row'))  40.5 us
    pallas_call x1, Pallas kernels, prep(): pl.pallas_call(prep_kernel, grid_spec=pltpu.PrefetchScalarGridSpec(num_sc...  25.4 us
  transfers between devices with their start and end apart: 6, of which 5 were waited for; matrix products, arithmetic and copies ran while one was open for 2% of the time, Pallas kernels for 12%

profile of v1, /device:TPU:0, one launch (start us, length us, event | category | flops | bytes accessed | tf_op | source)
XLA Modules:
  0.0 1035.2 jit_solution(10786744884997702805)
XLA Ops:
  7.2 0.0 all-gather.5.cloned.1.call-start
  7.2 1.5 slice_bitcast_fusion.4
  8.7 0.5 fusion
  9.2 1.3 copy.21
  10.6 0.0 all-gather.5.cloned.1.call-update
  10.6 0.0 all-gather.7.cloned.1.call-start
  10.6 1.3 copy.22
  12.0 0.0 all-gather.7.cloned.1.call-update
  12.0 0.0 all-reduce.5.cloned.1.call-start
  12.0 0.6 pad_add_fusion.pq_ref
  12.6 40.5 %all-gather.5.cloned.1.call-done = f32[512,3072]{1,0:T(8,128)} async-done(((f32[64,3072]{1,0:T(8,128)}), f32[512,3072]{1,0:T(8,128)}) %all-gather.5.cloned.1.call-update) | async-done | bytes 6291472 | tf_op jit(solution)/shard_map/all_gather | solution.py:532
  53.1 8.5 interleave.2
  61.6 6.2 slice_bitcast_fusion.2
  67.9 37.4 %panel_qr0.1 = (f32[64,12288]{1,0:T(8,128)}, bf16[192,12288]{1,0:T(8,128)(2,1)}, f32[128,64]{1,0:T(8,128)}, f32[64,64]{1,0:T(8,128)}) custom-call(f32[64,12288]{1,0:T(8,128)} %get-tuple-element.83.p_ref), custom_call_target="tpu_custom_call" | custom-call | tf_op jit(solution)/shard_map/panel_qr0/pallas_call | solution.py:223
  105.3 71.1 %times_matrix.4 = (f32[64,12288]{1,0:T(8,128)}, f32[64,3072]{1,0:T(8,128)}) custom-call(s32[21]{0:T(128)} %constant.13.clone.ti_ref, s32[21]{0:T(128)} %constant.14.clone.tj_ref, s32[2]{0:T(128)} %pad_add_fusion.pq_ref, f32[3072,6144]{1,0:T(8,128)} %bitcast.2.l_ref, bf16[192,12288]{1,0:T(8,128)(2,1)} %get-tuple-element.37.vtc_ref.refs_2_, ...), custom_call_target="tpu_custom_call" | custom-call | tf_op jit(solution)/shard_map/times_matrix/pallas_call | solution.py:323
  176.4 0.0 all-reduce.5.cloned.1.call-update
  176.4 0.3 all-reduce.7.cloned.1.call-start
  176.8 0.0 all-gather.7.cloned.1.call-done
  176.8 8.6 interleave.3
  185.4 49.2 %all-reduce.5.cloned.1.call-done.refs_0_ = f32[64,12288]{1,0:T(8,128)} async-done(((f32[64,12288]{1,0:T(8,128)}), f32[64,12288]{1,0:T(8,128)}) %all-reduce.5.cloned.1.call-update) | async-done | bytes 3145744 | tf_op jit(solution)/shard_map/psum | solution.py:540
  234.6 24.6 %make_w0.1 = (f32[64,12288]{1,0:T(8,128)}, f32[64,12288]{1,0:T(8,128)}) custom-call(f32[64,12288]{1,0:T(8,128)} %all-reduce.5.cloned.1.call-done.refs_0_, f32[64,12288]{1,0:T(8,128)} %get-tuple-element.36.vtp_ref.refs_1_.refs_4_.refs_0_.refs_8_, bf16[192,12288]{1,0:T(8,128)(2,1)} %get-tuple-element.37.vtc_ref.refs_2_, f32[64,64]{1,0:T(8,128)} %get-tuple-element.39.refs_3_, ...), custom_call_target="tpu_custom_call" | custom-call | tf_op jit(solution)/shard_map/make_w0/pallas_call | solution.py:430
  259.2 37.4 %panel_qr1.1 = (f32[64,12288]{1,0:T(8,128)}, bf16[192,12288]{1,0:T(8,128)(2,1)}, f32[128,64]{1,0:T(8,128)}, f32[64,64]{1,0:T(8,128)}) custom-call(f32[64,12288]{1,0:T(8,128)} %get-tuple-element.40.p_ref), custom_call_target="tpu_custom_call" | custom-call | tf_op jit(solution)/shard_map/panel_qr1/pallas_call | solution.py:223
  296.6 71.1 %times_matrix.5 = (f32[64,12288]{1,0:T(8,128)}, f32[64,3072]{1,0:T(8,128)}) custom-call(s32[21]{0:T(128)} %constant.13.clone.ti_ref, s32[21]{0:T(128)} %constant.14.clone.tj_ref, s32[2]{0:T(128)} %pad_add_fusion.pq_ref, f32[3072,6144]{1,0:T(8,128)} %bitcast.2.l_ref, bf16[192,12288]{1,0:T(8,128)(2,1)} %get-tuple-element.42.vtc_ref.refs_2_, ...), custom_call_target="tpu_custom_call" | custom-call | tf_op jit(solution)/shard_map/times_matrix/pallas_call | solution.py:323
  367.8 0.0 all-reduce.7.cloned.1.call-update
  367.8 0.6 all-reduce.9.cloned.1.call-start
  368.4 6.2 slice_bitcast_fusion
  374.6 51.4 %all-reduce.7.cloned.1.call-done.refs_0_ = f32[64,12288]{1,0:T(8,128)} async-done(((f32[64,12288]{1,0:T(8,128)}), f32[64,12288]{1,0:T(8,128)}) %all-reduce.7.cloned.1.call-update) | async-done | bytes 3145744 | tf_op jit(solution)/shard_map/psum | solution.py:540
  426.0 38.6 %make_w1.1 = (f32[64,12288]{1,0:T(8,128)}, f32[64,12288]{1,0:T(8,128)}) custom-call(f32[64,12288]{1,0:T(8,128)} %all-reduce.7.cloned.1.call-done.refs_0_, f32[64,12288]{1,0:T(8,128)} %get-tuple-element.41.vtp_ref.refs_1_.refs_6_.refs_9_, bf16[192,12288]{1,0:T(8,128)(2,1)} %get-tuple-element.42.vtc_ref.refs_2_, f32[64,64]{1,0:T(8,128)} %get-tuple-element.44.refs_3_, ...), custom_call_target="tpu_custom_call" | custom-call | tf_op jit(solution)/shard_map/make_w1/pallas_call | solution.py:430
  464.6 37.4 %panel_qr2.1 = (f32[64,12288]{1,0:T(8,128)}, bf16[192,12288]{1,0:T(8,128)(2,1)}, f32[128,64]{1,0:T(8,128)}, f32[64,64]{1,0:T(8,128)}) custom-call(f32[64,12288]{1,0:T(8,128)} %get-tuple-element.46.p_ref), custom_call_target="tpu_custom_call" | custom-call | tf_op jit(solution)/shard_map/panel_qr2/pallas_call | solution.py:223
  502.0 71.2 %times_matrix.6 = (f32[64,12288]{1,0:T(8,128)}, f32[64,3072]{1,0:T(8,128)}) custom-call(s32[21]{0:T(128)} %constant.13.clone.ti_ref, s32[21]{0:T(128)} %constant.14.clone.tj_ref, s32[2]{0:T(128)} %pad_add_fusion.pq_ref, f32[3072,6144]{1,0:T(8,128)} %bitcast.2.l_ref, bf16[192,12288]{1,0:T(8,128)(2,1)} %get-tuple-element.48.vtc_ref.refs_2_, ...), custom_call_target="tpu_custom_call" | custom-call | tf_op jit(solution)/shard_map/times_matrix/pallas_call | solution.py:323
  573.2 0.0 all-reduce.9.cloned.1.call-update
  573.3 0.2 all-reduce.11.cloned.1.call-start
  573.5 58.0 %all-reduce.9.cloned.1.call-done.refs_0_ = f32[64,12288]{1,0:T(8,128)} async-done(((f32[64,12288]{1,0:T(8,128)}), f32[64,12288]{1,0:T(8,128)}) %all-reduce.9.cloned.1.call-update) | async-done | bytes 3145744 | tf_op jit(solution)/shard_map/psum | solution.py:540
  631.4 52.5 %make_w2.1 = (f32[64,12288]{1,0:T(8,128)}, f32[64,12288]{1,0:T(8,128)}) custom-call(f32[64,12288]{1,0:T(8,128)} %all-reduce.9.cloned.1.call-done.refs_0_, f32[64,12288]{1,0:T(8,128)} %get-tuple-element.47.vtp_ref.refs_1_.refs_8_.refs_2_.refs_10_, bf16[192,12288]{1,0:T(8,128)(2,1)} %get-tuple-element.48.vtc_ref.refs_2_, f32[64,64]{1,0:T(8,128)} %get-tuple-element.50.refs_3_, ...), custom_call_target="tpu_custom_call" | custom-call | tf_op jit(solution)/shard_map/make_w2/pallas_call | solution.py:430
  683.9 37.4 %panel_qr3.1 = (f32[64,12288]{1,0:T(8,128)}, bf16[192,12288]{1,0:T(8,128)(2,1)}, f32[128,64]{1,0:T(8,128)}, f32[64,64]{1,0:T(8,128)}) custom-call(f32[64,12288]{1,0:T(8,128)} %get-tuple-element.52.p_ref), custom_call_target="tpu_custom_call" | custom-call | tf_op jit(solution)/shard_map/panel_qr3/pallas_call | solution.py:223
  721.4 71.2 %times_matrix.7 = (f32[64,12288]{1,0:T(8,128)}, f32[64,3072]{1,0:T(8,128)}) custom-call(s32[21]{0:T(128)} %constant.13.clone.ti_ref, s32[21]{0:T(128)} %constant.14.clone.tj_ref, s32[2]{0:T(128)} %pad_add_fusion.pq_ref, f32[3072,6144]{1,0:T(8,128)} %bitcast.2.l_ref, bf16[192,12288]{1,0:T(8,128)(2,1)} %get-tuple-element.55.vtc_ref.refs_2_, ...), custom_call_target="tpu_custom_call" | custom-call | tf_op jit(solution)/shard_map/times_matrix/pallas_call | solution.py:323
  792.6 0.0 copy-start.3
  792.6 0.0 all-reduce.11.cloned.1.call-update
  792.6 1.1 pad_maximum_fusion
  793.7 0.8 copy.23
  794.5 0.0 copy-done.7
  794.5 0.7 pad_maximum_fusion.1
  795.2 0.0 copy-done.3
  795.2 1.9 maximum_bitcast_fusion
  797.1 53.7 %all-reduce.11.cloned.1.call-done.refs_0_ = f32[64,12288]{1,0:T(8,128)} async-done(((f32[64,12288]{1,0:T(8,128)}), f32[64,12288]{1,0:T(8,128)}) %all-reduce.11.cloned.1.call-update) | async-done | bytes 3145744 | tf_op jit(solution)/shard_map/psum | solution.py:540
  850.8 44.5 %make_w3.1.refs_7_.refs_15_ = f32[64,12288]{1,0:T(8,128)} custom-call(f32[64,12288]{1,0:T(8,128)} %all-reduce.11.cloned.1.call-done.refs_0_, f32[64,12288]{1,0:T(8,128)} %get-tuple-element.53.vtp_ref.refs_1_.refs_3_.refs_11_, bf16[192,12288]{1,0:T(8,128)(2,1)} %get-tuple-element.55.vtc_ref.refs_2_, f32[64,64]{1,0:T(8,128)} %get-tuple-element.57.refs_3_, ...), custom_call_target="tpu_custom_call" | custom-call | tf_op jit(solution)/shard_map/make_w3/pallas_call | solution.py:430
  895.3 25.4 %prep.1 = (bf16[3,3072,512]{2,1,0:T(8,128)(2,1)}, bf16[3,512,6144]{2,1,0:T(8,128)(2,1)}) custom-call(s32[2]{0:T(128)} %pad_add_fusion.pq_ref, f32[64,12288]{1,0:T(8,128)} %get-tuple-element.36.vtp_ref.refs_1_.refs_4_.refs_0_.refs_8_, f32[64,12288]{1,0:T(8,128)} %get-tuple-element.41.vtp_ref.refs_1_.refs_6_.refs_9_, ...), custom_call_target="tpu_custom_call" | custom-call | tf_op jit(solution)/shard_map/prep/pallas_call | solution.py:465
  920.7 107.5 %final_update.1 = f32[3072,6144]{1,0:T(8,128)} custom-call(s32[2]{0:T(128)} %pad_add_fusion.pq_ref, f32[3072,6144]{1,0:T(8,128)} %bitcast.2.l_ref, bf16[3,3072,512]{2,1,0:T(8,128)(2,1)} %get-tuple-element.58.x_ref, bf16[3,512,6144]{2,1,0:T(8,128)(2,1)} %get-tuple-element.59.y_ref), custom_call_target="tpu_custom_call" | custom-call | tf_op jit(solution)/shard_map/final_update/pallas_call | solution.py:507
  (13 shorter events, 0.0 us)
Async XLA Ops:
  7.2 45.9 %all-gather.5.cloned.1.call-start = ((), (), s32[]{:S(2)}) async-start(), calls=%async_computation.4 | async-start | bytes 7077888 | tf_op jit(solution)/shard_map/all_gather | solution.py:532
  10.6 166.2 %all-gather.7.cloned.1.call-start = ((), (), s32[]{:S(2)}) async-start(), calls=%async_computation.5 | async-start | bytes 7077888 | tf_op jit(solution)/shard_map/all_gather | solution.py:532
  12.0 222.6 %all-reduce.5.cloned.1.call-start = ((), (), s32[]{:S(2)}) async-start(), calls=%async_computation | async-start | bytes 6291456 | tf_op jit(solution)/shard_map/psum | solution.py:540
  176.4 249.6 %all-reduce.7.cloned.1.call-start = ((), (), s32[]{:S(2)}) async-start(), calls=%async_computation.1 | async-start | bytes 6291456 | tf_op jit(solution)/shard_map/psum | solution.py:540
  367.8 263.6 %all-reduce.9.cloned.1.call-start = ((), (), s32[]{:S(2)}) async-start(), calls=%async_computation.2 | async-start | bytes 6291456 | tf_op jit(solution)/shard_map/psum | solution.py:540
  573.3 277.6 %all-reduce.11.cloned.1.call-start = ((), (), s32[]{:S(2)}) async-start(), calls=%async_computation.3 | async-start | bytes 6291456 | tf_op jit(solution)/shard_map/psum | solution.py:540
  792.5 2.0 copy-start.4
  792.5 2.0 copy-start.5
  792.5 2.0 copy-start.6
  792.5 2.0 copy-start.7
  792.6 2.6 copy-start
  792.6 2.6 copy-start.1
  792.6 2.6 copy-start.2
  792.6 2.6 copy-start.3
Sparse Core Ops, SparseCore 0:
  10.7 42.3 all-gather.4
  54.9 39.6 all-gather.6
  176.6 58.0 all-reduce.4
  367.9 58.0 all-reduce.6
  573.4 58.0 all-reduce.8
  792.7 58.0 all-reduce.10

commit v2 on v1

v2 whole, which is shorter than its diff:
```python
import functools

import jax
import jax.numpy as jnp
from jax import lax
from jax.experimental import pallas as pl
from jax.experimental.pallas import tpu as pltpu
from jax.sharding import PartitionSpec as P

PANELS = 4
NB = 64
NB3 = 3 * NB
LANES = 128
N = 12288
HALF = N // 2
ROWS = N // 4
F32 = jnp.float32
BF16 = jnp.bfloat16
CH = 2048
NCH = N // CH
TR, TC = 512, 1024
NT = ROWS // TR
VMEM_LIMIT = 62 * 1024 * 1024


def lane_of_block(blk):
    pos = (blk % 2) * HALF + (blk // 2) * NB
    return pos // LANES, pos % LANES


def span(start, size):
    return pl.ds(pl.multiple_of(start, size), size)


def split3(x):
    x1 = x.astype(BF16)
    r = x - x1.astype(F32)
    x2 = r.astype(BF16)
    x3 = (r - x2.astype(F32)).astype(BF16)
    return x1, x2, x3


def dot_nn(a, b):
    return lax.dot_general(a, b, (((1,), (0,)), ((), ())), preferred_element_type=F32)


def dot_nt(a, b):
    return lax.dot_general(a, b, (((1,), (1,)), ((), ())), preferred_element_type=F32)


def hi_nn(a, b):
    return lax.dot_general(a, b, (((1,), (0,)), ((), ())), precision=lax.Precision.HIGHEST, preferred_element_type=F32)


def hi_tn(a, b):
    return lax.dot_general(a, b, (((0,), (0,)), ((), ())), precision=lax.Precision.HIGHEST, preferred_element_type=F32)


def stack3(x):
    return jnp.concatenate(split3(x), axis=0)


def fold9(acc):
    r = acc[0:NB] + (acc[NB:LANES] + acc[LANES:NB3])
    return r[:, 0:NB] + (r[:, NB:LANES] + r[:, LANES:NB3])


def iota2(shape, dim):
    return lax.broadcasted_iota(jnp.int32, shape, dim)


def params(**kw):
    return pltpu.CompilerParams(vmem_limit_bytes=VMEM_LIMIT, **kw)


PIECE = ROWS // 2


def interleave_kernel(a_ref, b_ref, o_ref):
    lo = iota2((NB, LANES), 1) < NB
    for m in range(PIECE // LANES):
        a = a_ref[0, :, m * LANES:(m + 1) * LANES]
        b = b_ref[0, :, m * LANES:(m + 1) * LANES]
        at = 2 * m * LANES
        o_ref[:, at:at + LANES] = jnp.where(lo, a, pltpu.roll(b, NB, 1))
        o_ref[:, at + LANES:at + 2 * LANES] = jnp.where(lo, pltpu.roll(a, NB, 1), b)


def interleave(gathered):
    return pl.pallas_call(
        interleave_kernel,
        grid=(2, 2),
        in_specs=[
            pl.BlockSpec((1, NB, PIECE), lambda c, m: (m * 4 + c, 0, 0)),
            pl.BlockSpec((1, NB, PIECE), lambda c, m: (m * 4 + c + 2, 0, 0)),
        ],
        out_specs=pl.BlockSpec((NB, 2 * PIECE), lambda c, m: (0, c * 2 + m)),
        out_shape=jax.ShapeDtypeStruct((NB, N), F32),
        compiler_params=params(),
        name="interleave",
    )(gathered, gathered)


def qr_kernel(k, p_ref, vts_ref, band_ref, t_ref, vt_ref, xb_ref, rt_ref, inv_ref, tau_ref, gram_ref):
    piv_tile, piv_off = lane_of_block(k + 1)
    diag_tile, diag_off = lane_of_block(k)
    piv = slice(piv_tile * LANES, piv_tile * LANES + LANES)

    def copy_in(c, _):
        at = span(c * CH, CH)
        vt_ref[:, at] = p_ref[:, at]
        return 0

    lax.fori_loop(0, NCH, copy_in, 0)
    lane64 = iota2((NB, LANES), 1)
    row64 = iota2((NB, LANES), 0)
    for cls in range(2):
        sl = slice(cls * HALF, cls * HALF + LANES)
        blk = 2 * (lane64 // NB) + cls
        vt_ref[:, sl] = jnp.where(blk >= k + 1, p_ref[:, sl], 0.0)
    rt_ref[...] = jnp.zeros_like(rt_ref)
    inv_ref[...] = jnp.zeros_like(inv_ref)
    tau_ref[...] = jnp.zeros_like(tau_ref)

    for g0 in range(8):
        r0 = 8 * g0
        groups = 8 - g0
        height = 8 * groups
        lane = iota2((height, LANES), 1)
        row_b = r0 + iota2((height, LANES), 0)
        row1 = r0 + iota2((height, 1), 0)

        def step(jj, _, r0=r0, groups=groups, height=height, lane=lane, row_b=row_b, row1=row1):
            j = r0 + jj
            at_piv = lane == piv_off + j

            def dots(c, accs):
                at = span(c * CH, CH)
                xb = jnp.broadcast_to(vt_ref[pl.ds(j, 1), at], (8, CH))
                xb_ref[:, at] = xb
                out = []
                for g in range(groups):
                    prod = vt_ref[r0 + 8 * g:r0 + 8 * g + 8, at] * xb
                    parts = [prod[:, t * LANES:(t + 1) * LANES] for t in range(CH // LANES)]
                    while len(parts) > 1:
                        parts = [parts[i] + parts[i + 1] for i in range(0, len(parts), 2)]
                    out.append(accs[g] + parts[0])
                return tuple(out)

            accs = lax.fori_loop(0, NCH, dots, tuple(jnp.zeros((8, LANES), F32) for _ in range(groups)))
            d = jnp.sum(jnp.concatenate(accs, axis=0), axis=1, keepdims=True)
            pv = jnp.sum(jnp.where(at_piv, vt_ref[r0:NB, piv], 0.0), axis=1, keepdims=True)
            is_j = row1 == j
            nrm2 = jnp.sum(jnp.where(is_j, d, 0.0), axis=0, keepdims=True)
            alpha = jnp.sum(jnp.where(is_j, pv, 0.0), axis=0, keepdims=True)
            norm = jnp.sqrt(nrm2)
            beta = jnp.where(alpha >= 0.0, -norm, norm)
            tau = (beta - alpha) / beta
            inv = 1.0 / (alpha - beta)
            proj = inv * (d - beta * pv)
            s = jnp.where(row1 > j, tau * proj * inv, 0.0)
            xb_ref[:, piv] = xb_ref[:, piv] - jnp.where(lane[0:8] == piv_off + j, beta, 0.0)
            sb = jnp.broadcast_to(s, (height, LANES))

            def update(c, _):
                at = span(c * CH, CH)
                xb = xb_ref[:, at]
                for g in range(groups):
                    sg = sb[8 * g:8 * g + 8]
                    blk = vt_ref[r0 + 8 * g:r0 + 8 * g + 8, at]
                    vt_ref[r0 + 8 * g:r0 + 8 * g + 8, at] = jnp.concatenate(
                        [blk[:, t * LANES:(t + 1) * LANES] - sg * xb[:, t * LANES:(t + 1) * LANES] for t in range(CH // LANES)], axis=1)
                return 0

            lax.fori_loop(0, NCH, update, 0)
            r_col = jnp.where(is_j, beta, jnp.where(row1 > j, pv - s * (alpha - beta), 0.0))
            rt_ref[r0:NB] = jnp.where(lane == j, r_col, rt_ref[r0:NB])
            vt_ref[r0:NB, piv] = jnp.where(at_piv & (row_b > j), 0.0, vt_ref[r0:NB, piv])
            inv_ref[r0:NB] = jnp.where(row_b == j, inv, inv_ref[r0:NB])
            tau_ref[r0:NB] = jnp.where(row_b == j, tau, tau_ref[r0:NB])
            return 0

        lax.fori_loop(0, 8, step, 0)

    vt_ref[:, piv] = jnp.where(lane64 == piv_off + row64, 0.0, vt_ref[:, piv])
    inv_b = inv_ref[...]
    gram_ref[...] = jnp.zeros_like(gram_ref)

    def finish(c, _):
        at = span(c * CH, CH)
        blk = vt_ref[:, at]
        blk = jnp.concatenate([blk[:, t * LANES:(t + 1) * LANES] * inv_b for t in range(CH // LANES)], axis=1)
        lanes = c * CH + iota2((NB, CH), 1)
        blk = jnp.where(lanes == piv_tile * LANES + piv_off + iota2((NB, CH), 0), 1.0, blk)
        st = stack3(blk)
        vts_ref[:, at] = st
        gram_ref[...] += dot_nt(st, st)
        return 0

    lax.fori_loop(0, NCH, finish, 0)
    gram = fold9(gram_ref[...])
    rr = iota2((NB, NB), 0)
    cc = iota2((NB, NB), 1)
    t_mat = jnp.where(rr == cc, tau_ref[:, 0:NB], 0.0)
    size = 1
    while size < NB:
        pair = (rr // (2 * size) == cc // (2 * size)) & ((rr // size) % 2 == 0) & ((cc // size) % 2 == 1)
        t_mat = t_mat - hi_nn(t_mat, hi_nn(jnp.where(pair, gram, 0.0), t_mat))
        size *= 2
    t_ref[...] = t_mat
    diag = p_ref[:, diag_tile * LANES:diag_tile * LANES + LANES].T[diag_off:diag_off + NB]
    band_ref[0:NB] = jnp.where(rr >= cc, diag, 0.0)
    band_ref[NB:LANES] = rt_ref[...].T[0:NB]


def panel_qr(k, panel):
    return pl.pallas_call(
        functools.partial(qr_kernel, k),
        out_shape=(
            jax.ShapeDtypeStruct((NB3, N), BF16),
            jax.ShapeDtypeStruct((LANES, NB), F32),
            jax.ShapeDtypeStruct((NB, NB), F32),
        ),
        scratch_shapes=[
            pltpu.VMEM((NB, N), F32),
            pltpu.VMEM((8, N), F32),
            pltpu.VMEM((NB, LANES), F32),
            pltpu.VMEM((NB, LANES), F32),
            pltpu.VMEM((NB, LANES), F32),
            pltpu.VMEM((NB3, NB3), F32),
        ],
        compiler_params=params(),
        cost_estimate=cost(200),
        name=f"panel_qr{k}",
    )(panel)


LOWER_TILES = [(i, j) for i in range(NT) for j in range(i + 1)]


def whole(ref_tile):
    return (ref_tile[0:NB].astype(F32) + ref_tile[NB:2 * NB].astype(F32)) + ref_tile[2 * NB:NB3].astype(F32)


def av_kernel(ti_ref, tj_ref, pq_ref, l_ref, vtc_ref, vtp_ref, z_ref, vrt_ref, vr_ref, ls_ref, vtr_ref, acc1_ref, acc2_ref):
    step = pl.program_id(0)
    ti = ti_ref[step]
    tj = tj_ref[step]
    proc_row = pq_ref[0]
    proc_col = pq_ref[1]
    upper = (proc_row >> 1) == 1

    @pl.when(step == 0)
    def _():
        acc1_ref[...] = jnp.zeros_like(acc1_ref)
        acc2_ref[...] = jnp.zeros_like(acc2_ref)

        def pick(i, _):
            tile = whole(vtp_ref[:, span(i * LANES, LANES)]).T
            vr_ref[span(i * NB, NB), :] = jnp.where(upper, tile[NB:LANES], tile[0:NB])
            return 0

        lax.fori_loop(0, HALF // LANES, pick, 0)

        def back(m, _):
            tile = vr_ref[span(m * LANES, LANES), :].T
            vrt_ref[:, span(m * LANES, LANES)] = tile
            vtr_ref[:, span(m * LANES, LANES)] = stack3(tile)
            return 0

        lax.fori_loop(0, ROWS // LANES, back, 0)

    cols = span(tj * TC, TC)
    rows = span(ti * TR, TR)
    vc = vtc_ref[:, cols]
    vr = vtr_ref[:, rows]
    pieces = 4
    size = TR // pieces
    for piece in range(pieces):
        sub = slice(piece * size, (piece + 1) * size)
        parts = split3(l_ref[sub, :])
        for n, part in enumerate(parts):
            ls_ref[n, sub, :] = part
        at = span(ti * TR + piece * size, size)
        acc1_ref[at, :] += dot_nt(parts[0], vc) + (dot_nt(parts[1], vc) + dot_nt(parts[2], vc))
    acc2_ref[:, cols] += dot_nn(vr, ls_ref[0])
    acc2_ref[0:2 * NB, cols] += dot_nn(vr[0:2 * NB], ls_ref[1])
    acc2_ref[0:NB, cols] += dot_nn(vr[0:NB], ls_ref[2])

    @pl.when(ti == tj)
    def _():
        diff = proc_row - proc_col
        row = iota2((NB, LANES), 0)
        lane = iota2((NB, LANES), 1)
        on = ((diff & 1) == 0) & (lane == row + (diff >> 1) * NB)
        for i in range(TR // NB):
            tile = l_ref[i * NB:(i + 1) * NB, i * LANES:(i + 1) * LANES]
            diag = jnp.sum(jnp.where(on, tile, 0.0), axis=1, keepdims=True)
            at = span(ti * TR + i * NB, NB)
            acc1_ref[at, 0:NB] = acc1_ref[at, 0:NB] - diag * vr_ref[at, :]

    @pl.when(step == len(LOWER_TILES) - 1)
    def _():
        def out(i, _):
            at = span(i * LANES, LANES)
            blk = acc1_ref[span(i * NB, NB), :]
            blk = blk[:, 0:NB] + (blk[:, NB:2 * NB] + blk[:, 2 * NB:NB3])
            wide = jnp.concatenate([jnp.where(upper, 0.0, blk), jnp.where(upper, blk, 0.0)], axis=0).T
            own = acc2_ref[0:NB, at] + (acc2_ref[NB:2 * NB, at] + acc2_ref[2 * NB:NB3, at])
            for cls in range(2):
                z_ref[:, span(cls * HALF + i * LANES, LANES)] = (
                    jnp.where(proc_col == cls, own, 0.0) + jnp.where((proc_row & 1) == cls, wide, 0.0))
            return 0

        lax.fori_loop(0, HALF // LANES, out, 0)


def cost(mega):
    return pl.CostEstimate(flops=mega * 1000000, bytes_accessed=mega * 1000, transcendentals=0)


def times_matrix(pq, l_loc, vts):
    tile_i = jnp.array([t[0] for t in LOWER_TILES], jnp.int32)
    tile_j = jnp.array([t[1] for t in LOWER_TILES], jnp.int32)
    return pl.pallas_call(
        av_kernel,
        grid_spec=pltpu.PrefetchScalarGridSpec(
            num_scalar_prefetch=3,
            grid=(len(LOWER_TILES),),
            in_specs=[
                pl.BlockSpec((TR, TC), lambda s, ti, tj, pq: (ti[s], tj[s])),
                pl.BlockSpec((NB3, HALF), lambda s, ti, tj, pq: (0, pq[1])),
                pl.BlockSpec((NB3, HALF), lambda s, ti, tj, pq: (0, pq[0] & 1)),
            ],
            out_specs=[
                pl.BlockSpec((NB, N), lambda s, ti, tj, pq: (0, 0)),
                pl.BlockSpec((NB, ROWS), lambda s, ti, tj, pq: (0, 0)),
            ],
            scratch_shapes=[
                pltpu.VMEM((ROWS, NB), F32),
                pltpu.VMEM((3, TR, TC), BF16),
                pltpu.VMEM((NB3, ROWS), BF16),
                pltpu.VMEM((ROWS, NB3), F32),
                pltpu.VMEM((NB3, HALF), F32),
            ],
        ),
        out_shape=(jax.ShapeDtypeStruct((NB, N), F32), jax.ShapeDtypeStruct((NB, ROWS), F32)),
        compiler_params=params(),
        cost_estimate=cost(400),
        name="times_matrix",
    )(tile_i, tile_j, pq, l_loc, vts, vts)


WCH = 1024
NW = N // WCH


def mm6(lhs, m, b1, b2, b3):
    r1 = dot_nn(lhs, b1)
    r2 = dot_nn(lhs[0:2 * m], b2)
    r3 = dot_nn(lhs[0:m], b3)
    return r1[0:m] + ((r1[m:2 * m] + r2[0:m]) + (r1[2 * m:3 * m] + (r2[m:2 * m] + r3)))


def split_rows(tiles, s):
    return jnp.concatenate([t[s * NB:(s + 1) * NB] for t in tiles], axis=0)


def ahead_kernel(k, *refs):
    last = k == PANELS - 1
    count = 2 * k
    vts_ref, prev, refs = refs[0], refs[1:1 + count], refs[1 + count:]
    if last:
        d_ref, acc_ref, lhs_ref = refs
    else:
        at_piv, a0_ref, d_ref, p_ref, acc_ref, lhs_ref = refs[:count], *refs[count:]
    m = NB if last else 2 * NB
    phase = pl.program_id(0)
    chunk = pl.program_id(1)

    @pl.when((phase == 0) & (chunk == 0))
    def _():
        acc_ref[...] = jnp.zeros_like(acc_ref)

    @pl.when(phase == 0)
    def _():
        vs = vts_ref[...]
        for n in range(count):
            acc_ref[n] += dot_nt(prev[n][...], vs)

    @pl.when((phase == 1) & (chunk == 0))
    def _():
        _, off = lane_of_block(k + 1)
        for j in range(k):
            c_v, c_w = fold9(acc_ref[2 * j]), fold9(acc_ref[2 * j + 1])
            mat = jnp.concatenate([c_w, c_v], axis=0).T
            if not last:
                tile = jnp.concatenate([whole(at_piv[2 * j + 1][...]), whole(at_piv[2 * j][...])], axis=0)
                mat = jnp.concatenate([mat, tile.T[off:off + NB]], axis=0)
            lhs_ref[:, j * LANES:(j + 1) * LANES] = stack3(mat)

    @pl.when(phase == 1)
    def _():
        tiles = [ref[...] for ref in prev]
        res = mm6(lhs_ref[...], m, split_rows(tiles, 0), split_rows(tiles, 1), split_rows(tiles, 2))
        d_ref[...] = res[0:NB]
        if not last:
            p_ref[...] = a0_ref[...] - res[NB:2 * NB]


def ahead(k, vts, prev, a0_next):
    last = k == PANELS - 1
    m = NB if last else 2 * NB
    wide = pl.BlockSpec((NB3, WCH), lambda ph, c: (0, c))
    late = pl.BlockSpec((NB, WCH), lambda ph, c: (0, c * ph))
    tile, _ = lane_of_block(k + 1)
    piv = pl.BlockSpec((NB3, LANES), lambda ph, c: (0, tile))
    args = [vts, *prev] + ([] if last else [*prev, a0_next])
    res = pl.pallas_call(
        functools.partial(ahead_kernel, k),
        grid=(2, NW),
        in_specs=[wide] * (1 + 2 * k) + ([] if last else [piv] * (2 * k) + [late]),
        out_specs=[late] * (1 if last else 2),
        out_shape=[jax.ShapeDtypeStruct((NB, N), F32)] * (1 if last else 2),
        scratch_shapes=[pltpu.VMEM((2 * k, NB3, NB3), F32), pltpu.VMEM((3 * m, LANES * k), BF16)],
        compiler_params=params(),
        cost_estimate=cost(100 * k),
        name=f"ahead{k}",
    )(*args)
    return (res[0], None) if last else res


def w_kernel(k, *refs):
    last = k == PANELS - 1
    z_ref, vts_ref, t_ref = refs[:3]
    refs = refs[3:]
    if k > 0:
        d_ref, refs = refs[0], refs[1:]
    if last:
        wts_ref, zs_ref, acc_ref = refs
    else:
        a0_ref, wts_ref, p_ref, zs_ref, acc_ref = refs
    acc_ref[...] = jnp.zeros_like(acc_ref)

    def sums(c, _):
        at = span(c * WCH, WCH)
        z = z_ref[:, at]
        if k > 0:
            z = z - d_ref[:, at]
        zs = stack3(z)
        zs_ref[:, at] = zs
        acc_ref[...] += dot_nt(vts_ref[:, at], zs)
        return 0

    lax.fori_loop(0, NW, sums, 0)
    t_mat = t_ref[...]
    m_mat = hi_tn(t_mat, hi_nn(fold9(acc_ref[...]), t_mat))
    lhs = stack3(jnp.concatenate([t_mat, -0.5 * m_mat], axis=0).T)

    def write_w(c, _):
        at = span(c * WCH, WCH)
        tiles = [zs_ref[:, at], vts_ref[:, at]]
        w = mm6(lhs, NB, split_rows(tiles, 0), split_rows(tiles, 1), split_rows(tiles, 2))
        cls = c // (NW // 2)
        lane = (c - cls * (NW // 2)) * WCH + iota2((NB, WCH), 1)
        wts_ref[:, at] = stack3(jnp.where(2 * (lane // NB) + cls >= k + 1, w, 0.0))
        return 0

    lax.fori_loop(0, NW, write_w, 0)
    if last:
        return
    tile, off = lane_of_block(k + 1)
    piv = slice(tile * LANES, tile * LANES + LANES)
    both = jnp.concatenate([whole(wts_ref[:, piv]), whole(vts_ref[:, piv])], axis=0)
    lhs_p = stack3(both.T[off:off + NB])

    def write_p(c, _):
        at = span(c * WCH, WCH)
        tiles = [vts_ref[:, at], wts_ref[:, at]]
        p_ref[:, at] = a0_ref[:, at] - mm6(lhs_p, NB, split_rows(tiles, 0), split_rows(tiles, 1), split_rows(tiles, 2))
        return 0

    lax.fori_loop(0, NW, write_p, 0)


def make_w(k, z, vts, t_mat, d, a0_next):
    last = k == PANELS - 1
    args = [z, vts, t_mat] + ([d] if k > 0 else []) + ([] if last else [a0_next])
    outs = [jax.ShapeDtypeStruct((NB3, N), BF16)] + ([] if last else [jax.ShapeDtypeStruct((NB, N), F32)])
    res = pl.pallas_call(
        functools.partial(w_kernel, k),
        out_shape=tuple(outs),
        scratch_shapes=[pltpu.VMEM((NB3, N), BF16), pltpu.VMEM((NB3, NB3), F32)],
        compiler_params=params(),
        cost_estimate=cost(100),
        name=f"make_w{k}",
    )(*args)
    return (res[0], None) if last else res


PCH = 1024


def rows_kernel(pq_ref, a_ref, b_ref, x_ref):
    upper = (pq_ref[0] >> 1) == 1
    two = jnp.concatenate([whole(a_ref[...]), whole(b_ref[...])], axis=0).T
    for i in range(PCH // LANES):
        at = i * LANES
        half = jnp.where(upper, two[at + NB:at + LANES], two[at:at + NB])
        for s, part in enumerate(split3(half)):
            x_ref[s, i * NB:(i + 1) * NB, :] = part


def own_rows(pq, a, b):
    spec = pl.BlockSpec((NB3, PCH), lambda c, pq: (0, (pq[0] & 1) * (HALF // PCH) + c))
    return pl.pallas_call(
        rows_kernel,
        grid_spec=pltpu.PrefetchScalarGridSpec(
            num_scalar_prefetch=1,
            grid=(HALF // PCH,),
            in_specs=[spec] * 2,
            out_specs=pl.BlockSpec((3, PCH // 2, LANES), lambda c, pq: (0, c, 0)),
        ),
        out_shape=jax.ShapeDtypeStruct((3, ROWS, LANES), BF16),
        compiler_params=params(),
        cost_estimate=cost(20),
        name="own_rows",
    )(pq, a, b)


UPPER_TILES = [(i, j) for i in range(NT) for j in range(i + 1, NT)]


def final_order():
    order = []
    zeros = list(UPPER_TILES)
    for tile in LOWER_TILES:
        order.append(tile + tile)
        if zeros:
            order.append(tile + zeros.pop())
    return order


def final_kernel(tab_ref, pq_ref, l_ref, *refs):
    xs, ys, o_ref = refs[:4], refs[4:12], refs[12]
    step = pl.program_id(0)
    ti = tab_ref[2, step]
    tj = tab_ref[3, step]

    @pl.when(tj > ti)
    def _():
        o_ref[...] = jnp.zeros_like(o_ref)

    @pl.when(tj <= ti)
    def _():
        x1, x2, x3 = (jnp.concatenate([x[s] for x in xs], axis=1) for s in range(3))
        width = 256
        for c in range(TC // width):
            cols = slice(c * width, (c + 1) * width)
            tiles = [y[:, cols] for y in ys]
            y1, y2, y3 = (split_rows(tiles, s) for s in range(3))
            upd = dot_nn(x3, y1) + dot_nn(x1, y3) + dot_nn(x2, y2) + dot_nn(x2, y1) + dot_nn(x1, y2) + dot_nn(x1, y1)
            rloc = ti * TR + iota2((TR, width), 0)
            cloc = tj * TC + c * width + iota2((TR, width), 1)
            row = ((rloc // NB) * 4 + pq_ref[0]) * NB + rloc % NB
            col = ((cloc // NB) * 2 + pq_ref[1]) * NB + cloc % NB
            keep = (row >= col) & (col >= PANELS * NB)
            o_ref[:, cols] = jnp.where(keep, l_ref[:, cols] - upd, 0.0)


def final_update(pq, l_loc, xs, ys):
    order = final_order()
    table = jnp.array([[t[n] for t in order] for n in range(4)], jnp.int32)
    return pl.pallas_call(
        final_kernel,
        grid_spec=pltpu.PrefetchScalarGridSpec(
            num_scalar_prefetch=2,
            grid=(len(order),),
            in_specs=[pl.BlockSpec((TR, TC), lambda s, tab, pq: (tab[0, s], tab[1, s]))]
            + [pl.BlockSpec((3, TR, LANES), lambda s, tab, pq: (0, tab[0, s], 0))] * 4
            + [pl.BlockSpec((NB3, TC), lambda s, tab, pq: (0, pq[1] * (HALF // TC) + tab[1, s]))] * 8,
            out_specs=pl.BlockSpec((TR, TC), lambda s, tab, pq: (tab[2, s], tab[3, s])),
        ),
        out_shape=jax.ShapeDtypeStruct((ROWS, HALF), F32),
        compiler_params=params(),
        cost_estimate=cost(2000),
        name="final_update",
    )(table, pq, l_loc, *xs, *ys)


def first_panels(first, my_col):
    everyone = ("col", "row")
    out = []
    for h in range(2):
        own = first[NB * h:NB * h + NB]
        low, high = own[:, 0:PIECE], own[:, PIECE:ROWS]
        left = my_col == 0
        keep = jnp.where(left, low, high)
        got = lax.ppermute(jnp.where(left, high, low), "col", [(0, 1), (1, 0)])
        for mine in (jnp.where(left, keep, got), jnp.where(left, got, keep)):
            out.append(interleave(lax.all_gather(mine, everyone)))
    return out


def solution(mesh):
    mat_spec = P(("part", "row"), None, "col")

    def local_step(l_blk):
        l_loc = l_blk.reshape(ROWS, HALF)
        pq = jnp.stack([lax.axis_index("row"), lax.axis_index("col")]).astype(jnp.int32)
        panels0 = first_panels(l_loc[:, 0:LANES].T, lax.axis_index("col"))
        panel = panels0[0]
        prev = []
        v_list, w_list, band_list, vec_list, tri_list, xs = [], [], [], [], [], []
        for k in range(PANELS):
            vts, band, t_mat = panel_qr(k, panel)
            z_part, v_rows = times_matrix(pq, l_loc, vts)
            z = lax.psum(z_part, ("col", "row"))
            a0_next = panels0[k + 1] if k + 1 < PANELS else None
            d = None
            if k > 0:
                d, a0_next = ahead(k, vts, prev, a0_next)
            wts, panel = make_w(k, z, vts, t_mat, d, a0_next)
            prev = prev + [vts, wts]
            v_list.append(vts)
            w_list.append(wts)
            band_list.append(band)
            vec_list.append(v_rows)
            tri_list.append(t_mat)
        xs = [own_rows(pq, group[2 * n], group[2 * n + 1]) for group in (v_list, w_list) for n in range(2)]
        l_out = final_update(pq, l_loc, xs, w_list + v_list)
        return l_out.reshape(l_blk.shape), jnp.stack(band_list), jnp.stack(vec_list).transpose(0, 2, 1), jnp.stack(tri_list)

    return jax.shard_map(local_step, mesh=mesh, in_specs=(mat_spec,), out_specs=(mat_spec, P("part"), P(None, ("part", "row"), None), P("part")), check_vma=False)
```

time: 1040 us -> 975 us (0.938)
  waiting for transfers between devices: 253 us -> 145 us
  Pallas kernels: 744 us -> 789 us
    psum x4, waiting for transfers between devices: 212 us -> 103 us  [local_step(): z = lax.psum(z_part, ('col', 'row'))]
    pallas_call x3 -> x11, Pallas kernels: 42.5 us -> 133 us  [the longest x3 88.1 us: ahead(): pl.pallas_call(functools.partial(ahead_kernel, k), grid=(2, NW), in_specs...]
    pallas_call x4, Pallas kernels: 160 us -> 77.6 us  [make_w(): pl.pallas_call(functools.partial(w_kernel, k), out_shape=tuple(outs), scr...]
    pallas_call x1, Pallas kernels: 107 us -> 144 us  [final_update(): pl.pallas_call(final_kernel, grid_spec=pltpu.PrefetchScalarGridSpec(num_s...]
    ppermute x0 -> x2, waiting for transfers between devices: none -> 16.1 us  [first_panels(): got = lax.ppermute(jnp.where(left, high, low), 'col', [(0, 1), (1, 0)])]
    all_gather x2 -> x4, waiting for transfers between devices: 40.5 us -> 24.9 us  [first_panels(): out.append(interleave(lax.all_gather(mine, everyone)))]
    squeeze x2 -> x0, local copies, waits for them, and re-layouts: 12.5 us -> none  [local_step(): panels0 = [start[k // 2][k % 2] for k in range(PANELS)]]
  transfers between devices with their start and end apart: 6 -> 10, of which waited for: 5 -> 7; matrix products, arithmetic and copies ran while one was open for 2% -> 1% of each run, Pallas kernels for 12% -> 51%
where the time goes in v2:
time: 975 us; the launch traced here: 972 us
  Pallas kernels  789 us (81%)
  waiting for transfers between devices  145 us (15%)
  between operations  14.3 us (1%)
  local copies, waits for them, and re-layouts  11.5 us (1%)
    pallas_call x4, Pallas kernels, times_matrix(): pl.pallas_call(av_kernel, grid_spec=pltpu.PrefetchScalarGridSpec(num_scal...  286 us
    pallas_call x4, Pallas kernels, panel_qr(): pl.pallas_call(functools.partial(qr_kernel, k), out_shape=(jax.ShapeDtype...  148 us
    pallas_call x1, Pallas kernels, final_update(): pl.pallas_call(final_kernel, grid_spec=pltpu.PrefetchScalarGridSpec(num_s...  144 us
    psum x4, waiting for transfers between devices, local_step(): z = lax.psum(z_part, ('col', 'row'))  103 us
    pallas_call x3, Pallas kernels, ahead(): pl.pallas_call(functools.partial(ahead_kernel, k), grid=(2, NW), in_specs...  88.1 us
    pallas_call x4, Pallas kernels, make_w(): pl.pallas_call(functools.partial(w_kernel, k), out_shape=tuple(outs), scr...  77.6 us
    pallas_call x4, Pallas kernels, own_rows(): pl.pallas_call(rows_kernel, grid_spec=pltpu.PrefetchScalarGridSpec(num_sc...  26.2 us
    all_gather x4, waiting for transfers between devices, first_panels(): out.append(interleave(lax.all_gather(mine, everyone)))  24.9 us
  transfers between devices with their start and end apart: 10, of which 7 were waited for; matrix products, arithmetic and copies ran while one was open for 1% of the time, Pallas kernels for 51%

profile of v2, /device:TPU:0, one launch (start us, length us, event | category | flops | bytes accessed | tf_op | source)
XLA Modules:
  0.0 972.0 jit_solution(1471168600172593153)
XLA Ops:
  7.2 1.5 slice_bitcast_fusion
  8.7 0.5 slice_select_fusion
  9.2 0.2 copy.28
  9.5 3.4 collective-permute-start
  12.9 0.2 copy.33
  13.1 9.7 collective-permute-done
  22.8 1.2 copy.29
  24.0 6.4 collective-permute-done.1
  30.4 1.2 copy.34
  31.6 3.0 broadcast_select_fusion
  34.6 2.1 copy.30
  36.8 2.2 copy.32
  39.1 0.6 pad_add_fusion.pq_ref
  39.6 24.9 %all-gather.9.cloned.1.call-done = f32[512,1536]{1,0:T(8,128)} async-done(((f32[64,1536]{1,0:T(8,128)}), f32[512,1536]{1,0:T(8,128)}) %all-gather.9.cloned.1.call-update) | async-done | bytes 3145744 | tf_op jit(solution)/shard_map/all_gather | solution.py:601
  64.5 4.6 interleave.4.p_ref
  69.1 37.1 %panel_qr0.1 = (bf16[192,12288]{1,0:T(8,128)(2,1)}, f32[128,64]{1,0:T(8,128)}, f32[64,64]{1,0:T(8,128)}) custom-call(f32[64,12288]{1,0:T(8,128)} %interleave.4.p_ref), custom_call_target="tpu_custom_call" | custom-call | flops 200000000 | bytes 200000 | tf_op jit(solution)/shard_map/panel_qr0/pallas_call | solution.py:217
  106.2 71.6 %times_matrix.4 = (f32[64,12288]{1,0:T(8,128)}, f32[64,3072]{1,0:T(8,128)}) custom-call(s32[21]{0:T(128)} %constant.17.clone.ti_ref, s32[21]{0:T(128)} %constant.18.clone.tj_ref, s32[2]{0:T(128)} %pad_add_fusion.pq_ref, f32[3072,6144]{1,0:T(8,128)} %bitcast.2.l_ref, ...), custom_call_target="tpu_custom_call" | custom-call | flops 400000000 | bytes 400000 | tf_op jit(solution)/shard_map/times_matrix/pallas_call | solution.py:325
  177.8 1.0 copy.35
  178.9 0.2 all-reduce.7.cloned.1.call-start
  179.1 4.6 interleave.5.refs_3_
  183.7 52.2 %all-reduce.5.cloned.1.call-done.refs_0_ = f32[64,12288]{1,0:T(8,128)} async-done(((f32[64,12288]{1,0:T(8,128)}), f32[64,12288]{1,0:T(8,128)}) %all-reduce.5.cloned.1.call-update) | async-done | bytes 3145744 | tf_op jit(solution)/shard_map/psum | solution.py:618
  235.9 20.1 %make_w0.1 = (bf16[192,12288]{1,0:T(8,128)(2,1)}, f32[64,12288]{1,0:T(8,128)}) custom-call(f32[64,12288]{1,0:T(8,128)} %all-reduce.5.cloned.1.call-done.refs_0_, bf16[192,12288]{1,0:T(8,128)(2,1)} %get-tuple-element.34.vtc_ref.vtp_ref.refs_1_.a_ref.refs_3_.refs_5_.refs_8_, f32[64,64]{1,0:T(8,128)} %get-tuple-element.36.refs_2_, f32[64,12288]{1,0:T(8,128)} %interleave.5.refs_3_), custom_call_target="tpu_custom_call" | custom-call | flops 100000000 | bytes 100000 | tf_op jit(solution)/shard_map/make_w0/pallas_call | solution.py:490
  256.1 37.1 %panel_qr1.1 = (bf16[192,12288]{1,0:T(8,128)(2,1)}, f32[128,64]{1,0:T(8,128)}, f32[64,64]{1,0:T(8,128)}) custom-call(f32[64,12288]{1,0:T(8,128)} %get-tuple-element.37.p_ref), custom_call_target="tpu_custom_call" | custom-call | flops 200000000 | bytes 200000 | tf_op jit(solution)/shard_map/panel_qr1/pallas_call | solution.py:217
  293.2 71.5 %times_matrix.5 = (f32[64,12288]{1,0:T(8,128)}, f32[64,3072]{1,0:T(8,128)}) custom-call(s32[21]{0:T(128)} %constant.17.clone.ti_ref, s32[21]{0:T(128)} %constant.18.clone.tj_ref, s32[2]{0:T(128)} %pad_add_fusion.pq_ref, f32[3072,6144]{1,0:T(8,128)} %bitcast.2.l_ref, ...), custom_call_target="tpu_custom_call" | custom-call | flops 400000000 | bytes 400000 | tf_op jit(solution)/shard_map/times_matrix/pallas_call | solution.py:325
  364.8 1.0 copy.37
  366.0 4.6 interleave.6.refs_5_
  370.6 24.8 %ahead1.1 = (f32[64,12288]{1,0:T(8,128)}, f32[64,12288]{1,0:T(8,128)}) custom-call(bf16[192,12288]{1,0:T(8,128)(2,1)} %get-tuple-element.38.b_ref.vtc_ref.vtp_ref.refs_0_.refs_1_.refs_3_.refs_7_.refs_9_, bf16[192,12288]{1,0:T(8,128)(2,1)} %get-tuple-element.34.vtc_ref.vtp_ref.refs_1_.a_ref.refs_3_.refs_5_.refs_8_, ...), custom_call_target="tpu_custom_call" | custom-call | flops 100000000 | bytes 100000 | tf_op jit(solution)/shard_map/ahead1/pallas_call | solution.py:419
  395.3 27.7 %all-reduce.7.cloned.1.call-done.refs_0_ = f32[64,12288]{1,0:T(8,128)} async-done(((f32[64,12288]{1,0:T(8,128)}), f32[64,12288]{1,0:T(8,128)}) %all-reduce.7.cloned.1.call-update) | async-done | bytes 3145744 | tf_op jit(solution)/shard_map/psum | solution.py:618
  423.0 21.1 %make_w1.1 = (bf16[192,12288]{1,0:T(8,128)(2,1)}, f32[64,12288]{1,0:T(8,128)}) custom-call(f32[64,12288]{1,0:T(8,128)} %all-reduce.7.cloned.1.call-done.refs_0_, bf16[192,12288]{1,0:T(8,128)(2,1)} %get-tuple-element.38.b_ref.vtc_ref.vtp_ref.refs_0_.refs_1_.refs_3_.refs_7_.refs_9_, f32[64,64]{1,0:T(8,128)} %get-tuple-element.40.refs_2_, ...), custom_call_target="tpu_custom_call" | custom-call | flops 100000000 | bytes 100000 | tf_op jit(solution)/shard_map/make_w1/pallas_call | solution.py:490
  444.1 37.1 %panel_qr2.1 = (bf16[192,12288]{1,0:T(8,128)(2,1)}, f32[128,64]{1,0:T(8,128)}, f32[64,64]{1,0:T(8,128)}) custom-call(f32[64,12288]{1,0:T(8,128)} %get-tuple-element.44.p_ref), custom_call_target="tpu_custom_call" | custom-call | flops 200000000 | bytes 200000 | tf_op jit(solution)/shard_map/panel_qr2/pallas_call | solution.py:217
  481.3 71.5 %times_matrix.6 = (f32[64,12288]{1,0:T(8,128)}, f32[64,3072]{1,0:T(8,128)}) custom-call(s32[21]{0:T(128)} %constant.17.clone.ti_ref, s32[21]{0:T(128)} %constant.18.clone.tj_ref, s32[2]{0:T(128)} %pad_add_fusion.pq_ref, f32[3072,6144]{1,0:T(8,128)} %bitcast.2.l_ref, ...), custom_call_target="tpu_custom_call" | custom-call | flops 400000000 | bytes 400000 | tf_op jit(solution)/shard_map/times_matrix/pallas_call | solution.py:325
  552.8 0.3 all-reduce.11.cloned.1.call-start
  553.1 4.6 interleave.7.refs_9_
  557.7 29.9 %ahead2.1 = (f32[64,12288]{1,0:T(8,128)}, f32[64,12288]{1,0:T(8,128)}) custom-call(bf16[192,12288]{1,0:T(8,128)(2,1)} %get-tuple-element.45.vtc_ref.vtp_ref.refs_0_.refs_1_.a_ref.refs_5_.refs_10_, bf16[192,12288]{1,0:T(8,128)(2,1)} %get-tuple-element.34.vtc_ref.vtp_ref.refs_1_.a_ref.refs_3_.refs_5_.refs_8_, ...), custom_call_target="tpu_custom_call" | custom-call | flops 200000000 | bytes 200000 | tf_op jit(solution)/shard_map/ahead2/pallas_call | solution.py:419
  587.7 23.4 %all-reduce.9.cloned.1.call-done.refs_0_ = f32[64,12288]{1,0:T(8,128)} async-done(((f32[64,12288]{1,0:T(8,128)}), f32[64,12288]{1,0:T(8,128)}) %all-reduce.9.cloned.1.call-update) | async-done | bytes 3145744 | tf_op jit(solution)/shard_map/psum | solution.py:618
  611.0 21.1 %make_w2.1 = (bf16[192,12288]{1,0:T(8,128)(2,1)}, f32[64,12288]{1,0:T(8,128)}) custom-call(f32[64,12288]{1,0:T(8,128)} %all-reduce.9.cloned.1.call-done.refs_0_, bf16[192,12288]{1,0:T(8,128)(2,1)} %get-tuple-element.45.vtc_ref.vtp_ref.refs_0_.refs_1_.a_ref.refs_5_.refs_10_, f32[64,64]{1,0:T(8,128)} %get-tuple-element.47.refs_2_, ...), custom_call_target="tpu_custom_call" | custom-call | flops 100000000 | bytes 100000 | tf_op jit(solution)/shard_map/make_w2/pallas_call | solution.py:490
  632.2 37.1 %panel_qr3.1 = (bf16[192,12288]{1,0:T(8,128)(2,1)}, f32[128,64]{1,0:T(8,128)}, f32[64,64]{1,0:T(8,128)}) custom-call(f32[64,12288]{1,0:T(8,128)} %get-tuple-element.51.p_ref), custom_call_target="tpu_custom_call" | custom-call | flops 200000000 | bytes 200000 | tf_op jit(solution)/shard_map/panel_qr3/pallas_call | solution.py:217
  669.3 71.5 %times_matrix.7 = (f32[64,12288]{1,0:T(8,128)}, f32[64,3072]{1,0:T(8,128)}) custom-call(s32[21]{0:T(128)} %constant.17.clone.ti_ref, s32[21]{0:T(128)} %constant.18.clone.tj_ref, s32[2]{0:T(128)} %pad_add_fusion.pq_ref, f32[3072,6144]{1,0:T(8,128)} %bitcast.2.l_ref, bf16[192,12288]{1,0:T(8,128)(2,1)} %get-tuple-element.52.b_ref.vtc_ref.vtp_ref.refs_0_.refs_1_.refs_11_, ...), custom_call_target="tpu_custom_call" | custom-call | flops 400000000 | bytes 400000 | tf_op jit(solution)/shard_map/times_matrix/pallas_call | solution.py:325
  740.8 6.5 own_rows.4.refs_0_
  747.4 6.7 own_rows.6.refs_2_
  754.1 0.8 copy.38
  754.9 6.5 own_rows.5.refs_1_
  761.4 33.4 %ahead3.1.refs_3_ = f32[64,12288]{1,0:T(8,128)} custom-call(bf16[192,12288]{1,0:T(8,128)(2,1)} %get-tuple-element.52.b_ref.vtc_ref.vtp_ref.refs_0_.refs_1_.refs_11_, bf16[192,12288]{1,0:T(8,128)(2,1)} %get-tuple-element.34.vtc_ref.vtp_ref.refs_1_.a_ref.refs_3_.refs_5_.refs_8_, bf16[192,12288]{1,0:T(8,128)(2,1)} %get-tuple-element.41.refs_2_.refs_4_.refs_6_.a_ref, ...), custom_call_target="tpu_custom_call" | custom-call | flops 300000000 | bytes 300000 | tf_op jit(solution)/shard_map/ahead3/pallas_call | solution.py:419
  794.8 0.7 pad_maximum_fusion.1
  795.5 3.4 maximum_bitcast_fusion
  799.0 15.2 %make_w3.1.b_ref.refs_7_ = bf16[192,12288]{1,0:T(8,128)(2,1)} custom-call(f32[64,12288]{1,0:T(8,128)} %all-reduce.11.cloned.1.call-done.refs_0_, bf16[192,12288]{1,0:T(8,128)(2,1)} %get-tuple-element.52.b_ref.vtc_ref.vtp_ref.refs_0_.refs_1_.refs_11_, f32[64,64]{1,0:T(8,128)} %get-tuple-element.55.refs_2_, f32[64,12288]{1,0:T(8,128)} %ahead3.1.refs_3_), custom_call_target="tpu_custom_call" | custom-call | flops 100000000 | bytes 100000 | tf_op jit(solution)/shard_map/make_w3/pallas_call | solution.py:490
  814.2 6.5 own_rows.7.refs_3_
  820.8 144.4 %final_update.1 = f32[3072,6144]{1,0:T(8,128)} custom-call(s32[4,36]{1,0:T(4,128)} %constant.19.clone.tab_ref, s32[2]{0:T(128)} %pad_add_fusion.pq_ref, f32[3072,6144]{1,0:T(8,128)} %bitcast.2.l_ref, bf16[3,3072,128]{2,1,0:T(8,128)(2,1)} %own_rows.4.refs_0_, bf16[3,3072,128]{2,1,0:T(8,128)(2,1)} %own_rows.5.refs_1_, bf16[3,3072,128]{2,1,0:T(8,128)(2,1)} %own_rows.6.refs_2_, ...), custom_call_target="tpu_custom_call" | custom-call | flops 2000000000 | bytes 2000000 | tf_op jit(solution)/shard_map/final_update/pallas_call | solution.py:574
  (40 shorter events, 0.7 us)
Async XLA Ops:
  7.2 57.3 %all-gather.9.cloned.1.call-start = ((), (), s32[]{:S(2)}) async-start(), calls=%async_computation.4 | async-start | bytes 3538944 | tf_op jit(solution)/shard_map/all_gather | solution.py:601
  9.5 13.4 %collective-permute-start = (f32[64,1536]{1,0:T(8,128)S(1)}, f32[64,1536]{1,0:T(8,128)S(1)}, u32[]{:S(2)}, u32[]{:S(2)}) collective-permute-start(f32[64,1536]{1,0:T(8,128)S(1)} %copy.28), channel_id=1, source_target_pairs={{0,4},{4,0},{1,5},{5,1},{2,6},{6,2},{3,7},{7,3}} | collective-permute-start | bytes 1179656 | tf_op jit(solution)/shard_map/ppermute | solution.py:599
  13.1 17.3 %collective-permute-start.1 = (f32[64,1536]{1,0:T(8,128)S(1)}, f32[64,1536]{1,0:T(8,128)S(1)}, u32[]{:S(2)}, u32[]{:S(2)}) collective-permute-start(f32[64,1536]{1,0:T(8,128)S(1)} %copy.33), channel_id=1, source_target_pairs={{0,4},{4,0},{1,5},{5,1},{2,6},{6,2},{3,7},{7,3}} | collective-permute-start | bytes 1179656 | tf_op jit(solution)/shard_map/ppermute | solution.py:599
  36.8 142.3 %all-gather.11.cloned.1.call-start = ((), (), s32[]{:S(2)}) async-start(), calls=%async_computation.5 | async-start | bytes 3538944 | tf_op jit(solution)/shard_map/all_gather | solution.py:601
  39.0 196.9 %all-reduce.5.cloned.1.call-start = ((), (), s32[]{:S(2)}) async-start(), calls=%async_computation | async-start | bytes 6291456 | tf_op jit(solution)/shard_map/psum | solution.py:618
  177.8 188.2 %all-gather.13.cloned.1.call-start = ((), (), s32[]{:S(2)}) async-start(), calls=%async_computation.6 | async-start | bytes 3538944 | tf_op jit(solution)/shard_map/all_gather | solution.py:601
  178.9 244.2 %all-reduce.7.cloned.1.call-start = ((), (), s32[]{:S(2)}) async-start(), calls=%async_computation.1 | async-start | bytes 6291456 | tf_op jit(solution)/shard_map/psum | solution.py:618
  364.8 188.3 %all-gather.15.cloned.1.call-start = ((), (), s32[]{:S(2)}) async-start(), calls=%async_computation.7 | async-start | bytes 3538944 | tf_op jit(solution)/shard_map/all_gather | solution.py:601
  365.9 245.2 %all-reduce.9.cloned.1.call-start = ((), (), s32[]{:S(2)}) async-start(), calls=%async_computation.2 | async-start | bytes 6291456 | tf_op jit(solution)/shard_map/psum | solution.py:618
  552.8 246.2 %all-reduce.11.cloned.1.call-start = ((), (), s32[]{:S(2)}) async-start(), calls=%async_computation.3 | async-start | bytes 6291456 | tf_op jit(solution)/shard_map/psum | solution.py:618
  747.4 6.7 copy-start.6
  747.4 6.7 copy-start.7
  747.4 6.7 copy-start.8
  747.4 6.7 copy-start.9
  761.4 33.4 %copy-start.2 = (f32[64,64]{1,0:T(8,128)S(1)}, f32[64,64]{1,0:T(8,128)}, u32[]{:S(2)}) copy-start(f32[64,64]{1,0:T(8,128)} %get-tuple-element.36.refs_2_) | copy-start | bytes 49156
  761.4 33.4 %copy-start.3 = (f32[64,64]{1,0:T(8,128)S(1)}, f32[64,64]{1,0:T(8,128)}, u32[]{:S(2)}) copy-start(f32[64,64]{1,0:T(8,128)} %get-tuple-element.40.refs_2_) | copy-start | bytes 49156
  761.4 33.4 %copy-start.4 = (f32[64,64]{1,0:T(8,128)S(1)}, f32[64,64]{1,0:T(8,128)}, u32[]{:S(2)}) copy-start(f32[64,64]{1,0:T(8,128)} %get-tuple-element.47.refs_2_) | copy-start | bytes 49156
  761.4 33.4 %copy-start.5 = (f32[64,64]{1,0:T(8,128)S(1)}, f32[64,64]{1,0:T(8,128)}, u32[]{:S(2)}) copy-start(f32[64,64]{1,0:T(8,128)} %get-tuple-element.55.refs_2_) | copy-start | bytes 49156
  761.4 34.1 %copy-start = (f32[64,3072]{1,0:T(8,128)S(1)}, f32[64,3072]{1,0:T(8,128)}, u32[]{:S(2)}) copy-start(f32[64,3072]{1,0:T(8,128)} %get-tuple-element.60) | copy-start | bytes 2359300
  761.4 34.1 %copy-start.1 = (f32[64,3072]{1,0:T(8,128)S(1)}, f32[64,3072]{1,0:T(8,128)}, u32[]{:S(2)}) copy-start(f32[64,3072]{1,0:T(8,128)} %get-tuple-element.61) | copy-start | bytes 2359300
Sparse Core Ops, SparseCore 0:
  36.9 27.5 all-gather.8
  66.3 26.3 all-gather.10
  177.9 58.0 all-reduce.4
  237.6 26.4 all-gather.12
  364.9 58.0 all-reduce.6
  424.7 26.4 all-gather.14
  552.9 58.0 all-reduce.8
  741.0 58.0 all-reduce.10

commit v3 on v2

--- a/solution.py
+++ b/solution.py
@@ -19,6 +19,7 @@
 CH = 2048
 NCH = N // CH
 TR, TC = 512, 1024
+KW = 256
 NT = ROWS // TR
 VMEM_LIMIT = 62 * 1024 * 1024
 
@@ -242,7 +243,7 @@
     return (ref_tile[0:NB].astype(F32) + ref_tile[NB:2 * NB].astype(F32)) + ref_tile[2 * NB:NB3].astype(F32)
 
 
-def av_kernel(ti_ref, tj_ref, pq_ref, l_ref, vtc_ref, vtp_ref, z_ref, vrt_ref, vr_ref, ls_ref, vtr_ref, acc1_ref, acc2_ref):
+def av_kernel(ti_ref, tj_ref, pq_ref, l_ref, vtc_ref, vtp_ref, z_ref, vrt_ref, vr_ref, vtr_ref, acc1_ref, acc2_ref):
     step = pl.program_id(0)
     ti = ti_ref[step]
     tj = tj_ref[step]
@@ -270,22 +271,20 @@
 
         lax.fori_loop(0, ROWS // LANES, back, 0)
 
-    cols = span(tj * TC, TC)
     rows = span(ti * TR, TR)
-    vc = vtc_ref[:, cols]
     vr = vtr_ref[:, rows]
-    pieces = 4
-    size = TR // pieces
-    for piece in range(pieces):
-        sub = slice(piece * size, (piece + 1) * size)
-        parts = split3(l_ref[sub, :])
-        for n, part in enumerate(parts):
-            ls_ref[n, sub, :] = part
-        at = span(ti * TR + piece * size, size)
-        acc1_ref[at, :] += dot_nt(parts[0], vc) + (dot_nt(parts[1], vc) + dot_nt(parts[2], vc))
-    acc2_ref[:, cols] += dot_nn(vr, ls_ref[0])
-    acc2_ref[0:2 * NB, cols] += dot_nn(vr[0:2 * NB], ls_ref[1])
-    acc2_ref[0:NB, cols] += dot_nn(vr[0:NB], ls_ref[2])
+    for piece in range(TC // KW):
+        sub = slice(piece * KW, (piece + 1) * KW)
+        at = span(tj * TC + piece * KW, KW)
+        p1, p2, p3 = split3(l_ref[:, sub])
+        vc = vtc_ref[:, at]
+        acc1_ref[rows, :] += dot_nt(p1, vc) + (dot_nt(p2, vc) + dot_nt(p3, vc))
+        r1 = dot_nn(vr, p1)
+        r2 = dot_nn(vr[0:2 * NB], p2)
+        r3 = dot_nn(vr[0:NB], p3)
+        acc2_ref[0:NB, at] += (r1[0:NB] + r2[0:NB]) + r3
+        acc2_ref[NB:2 * NB, at] += r1[NB:2 * NB] + r2[NB:2 * NB]
+        acc2_ref[2 * NB:NB3, at] += r1[2 * NB:NB3]
 
     @pl.when(ti == tj)
     def _():
@@ -338,7 +337,6 @@
             ],
             scratch_shapes=[
                 pltpu.VMEM((ROWS, NB), F32),
-                pltpu.VMEM((3, TR, TC), BF16),
                 pltpu.VMEM((NB3, ROWS), BF16),
                 pltpu.VMEM((ROWS, NB3), F32),
                 pltpu.VMEM((NB3, HALF), F32),
@@ -501,7 +499,8 @@
 PCH = 1024
 
 
-def rows_kernel(pq_ref, a_ref, b_ref, x_ref):
+def place_kernel(pq_ref, a_ref, b_ref, ac_ref, bc_ref, *refs):
+    x_ref, y_ref = refs[-2:]
     upper = (pq_ref[0] >> 1) == 1
     two = jnp.concatenate([whole(a_ref[...]), whole(b_ref[...])], axis=0).T
     for i in range(PCH // LANES):
@@ -509,23 +508,31 @@
         half = jnp.where(upper, two[at + NB:at + LANES], two[at:at + NB])
         for s, part in enumerate(split3(half)):
             x_ref[s, i * NB:(i + 1) * NB, :] = part
-
-
-def own_rows(pq, a, b):
-    spec = pl.BlockSpec((NB3, PCH), lambda c, pq: (0, (pq[0] & 1) * (HALF // PCH) + c))
+    for s in range(3):
+        y_ref[s] = split_rows([ac_ref, bc_ref], s)
+
+
+def place(pq, old, pos, a, b):
+    blocks = HALF // PCH
+    row_spec = pl.BlockSpec((NB3, PCH), lambda c, pq: (0, (pq[0] & 1) * blocks + c))
+    col_spec = pl.BlockSpec((NB3, PCH), lambda c, pq: (0, pq[1] * blocks + c))
     return pl.pallas_call(
-        rows_kernel,
+        place_kernel,
         grid_spec=pltpu.PrefetchScalarGridSpec(
             num_scalar_prefetch=1,
-            grid=(HALF // PCH,),
-            in_specs=[spec] * 2,
-            out_specs=pl.BlockSpec((3, PCH // 2, LANES), lambda c, pq: (0, c, 0)),
+            grid=(blocks,),
+            in_specs=[row_spec] * 2 + [col_spec] * 2 + [pl.BlockSpec(memory_space=pl.ANY)] * len(old),
+            out_specs=[
+                pl.BlockSpec((3, PCH // 2, LANES), lambda c, pq: (0, c, pos)),
+                pl.BlockSpec((3, LANES, PCH), lambda c, pq: (0, (pos + 2) % 4, c)),
+            ],
         ),
-        out_shape=jax.ShapeDtypeStruct((3, ROWS, LANES), BF16),
+        out_shape=(jax.ShapeDtypeStruct((3, ROWS, 512), BF16), jax.ShapeDtypeStruct((3, 512, HALF), BF16)),
+        input_output_aliases={5: 0, 6: 1} if old else {},
         compiler_params=params(),
         cost_estimate=cost(20),
-        name="own_rows",
-    )(pq, a, b)
+        name="place",
+    )(pq, a, b, a, b, *old)
 
 
 UPPER_TILES = [(i, j) for i in range(NT) for j in range(i + 1, NT)]
@@ -541,8 +548,7 @@
     return order
 
 
-def final_kernel(tab_ref, pq_ref, l_ref, *refs):
-    xs, ys, o_ref = refs[:4], refs[4:12], refs[12]
+def final_kernel(tab_ref, pq_ref, l_ref, x_ref, y_ref, o_ref):
     step = pl.program_id(0)
     ti = tab_ref[2, step]
     tj = tab_ref[3, step]
@@ -553,12 +559,11 @@
 
     @pl.when(tj <= ti)
     def _():
-        x1, x2, x3 = (jnp.concatenate([x[s] for x in xs], axis=1) for s in range(3))
+        x1, x2, x3 = x_ref[0], x_ref[1], x_ref[2]
         width = 256
         for c in range(TC // width):
             cols = slice(c * width, (c + 1) * width)
-            tiles = [y[:, cols] for y in ys]
-            y1, y2, y3 = (split_rows(tiles, s) for s in range(3))
+            y1, y2, y3 = y_ref[0, :, cols], y_ref[1, :, cols], y_ref[2, :, cols]
             upd = dot_nn(x3, y1) + dot_nn(x1, y3) + dot_nn(x2, y2) + dot_nn(x2, y1) + dot_nn(x1, y2) + dot_nn(x1, y1)
             rloc = ti * TR + iota2((TR, width), 0)
             cloc = tj * TC + c * width + iota2((TR, width), 1)
@@ -568,7 +573,7 @@
             o_ref[:, cols] = jnp.where(keep, l_ref[:, cols] - upd, 0.0)
 
 
-def final_update(pq, l_loc, xs, ys):
+def final_update(pq, l_loc, x, y):
     order = final_order()
     table = jnp.array([[t[n] for t in order] for n in range(4)], jnp.int32)
     return pl.pallas_call(
@@ -576,25 +581,49 @@
         grid_spec=pltpu.PrefetchScalarGridSpec(
             num_scalar_prefetch=2,
             grid=(len(order),),
-            in_specs=[pl.BlockSpec((TR, TC), lambda s, tab, pq: (tab[0, s], tab[1, s]))]
-            + [pl.BlockSpec((3, TR, LANES), lambda s, tab, pq: (0, tab[0, s], 0))] * 4
-            + [pl.BlockSpec((NB3, TC), lambda s, tab, pq: (0, pq[1] * (HALF // TC) + tab[1, s]))] * 8,
+            in_specs=[
+                pl.BlockSpec((TR, TC), lambda s, tab, pq: (tab[0, s], tab[1, s])),
+                pl.BlockSpec((3, TR, 512), lambda s, tab, pq: (0, tab[0, s], 0)),
+                pl.BlockSpec((3, 512, TC), lambda s, tab, pq: (0, 0, tab[1, s])),
+            ],
             out_specs=pl.BlockSpec((TR, TC), lambda s, tab, pq: (tab[2, s], tab[3, s])),
         ),
         out_shape=jax.ShapeDtypeStruct((ROWS, HALF), F32),
         compiler_params=params(),
         cost_estimate=cost(2000),
         name="final_update",
-    )(table, pq, l_loc, *xs, *ys)
-
-
-def first_panels(first, my_col):
+    )(table, pq, l_loc, x, y)
+
+
+def first_kernel(l_ref, o_ref):
+    for m in range(PIECE // LANES):
+        tile = l_ref[m * LANES:(m + 1) * LANES, :].T
+        o_ref[0, :, m * LANES:(m + 1) * LANES] = tile[0:NB]
+        o_ref[1, :, m * LANES:(m + 1) * LANES] = tile[NB:LANES]
+
+
+def first_columns(l_loc):
+    return pl.pallas_call(
+        first_kernel,
+        grid=(2,),
+        in_specs=[pl.BlockSpec((PIECE, LANES), lambda m: (m, 0))],
+        out_specs=pl.BlockSpec((2, NB, PIECE), lambda m: (0, 0, m)),
+        out_shape=jax.ShapeDtypeStruct((2, NB, ROWS), F32),
+        compiler_params=params(),
+        name="first_columns",
+    )(l_loc)
+
+
+def first_panels(l_loc, my_col):
     everyone = ("col", "row")
+    both = first_columns(l_loc)
+    left = my_col == 0
     out = []
     for h in range(2):
-        own = first[NB * h:NB * h + NB]
+        own = both[h]
+        if out:
+            own, out[0] = lax.optimization_barrier((own, out[0]))
         low, high = own[:, 0:PIECE], own[:, PIECE:ROWS]
-        left = my_col == 0
         keep = jnp.where(left, low, high)
         got = lax.ppermute(jnp.where(left, high, low), "col", [(0, 1), (1, 0)])
         for mine in (jnp.where(left, keep, got), jnp.where(left, got, keep)):
@@ -608,10 +637,10 @@
     def local_step(l_blk):
         l_loc = l_blk.reshape(ROWS, HALF)
         pq = jnp.stack([lax.axis_index("row"), lax.axis_index("col")]).astype(jnp.int32)
-        panels0 = first_panels(l_loc[:, 0:LANES].T, lax.axis_index("col"))
+        panels0 = first_panels(l_loc, lax.axis_index("col"))
         panel = panels0[0]
         prev = []
-        v_list, w_list, band_list, vec_list, tri_list, xs = [], [], [], [], [], []
+        v_list, w_list, band_list, vec_list, tri_list = [], [], [], [], []
         for k in range(PANELS):
             vts, band, t_mat = panel_qr(k, panel)
             z_part, v_rows = times_matrix(pq, l_loc, vts)
@@ -627,8 +656,11 @@
             band_list.append(band)
             vec_list.append(v_rows)
             tri_list.append(t_mat)
-        xs = [own_rows(pq, group[2 * n], group[2 * n + 1]) for group in (v_list, w_list) for n in range(2)]
-        l_out = final_update(pq, l_loc, xs, w_list + v_list)
+        factors = ()
+        for pos, group in enumerate((v_list, v_list, w_list, w_list)):
+            n = 2 * (pos % 2)
+            factors = place(pq, factors, pos, group[n], group[n + 1])
+        l_out = final_update(pq, l_loc, *factors)
         return l_out.reshape(l_blk.shape), jnp.stack(band_list), jnp.stack(vec_list).transpose(0, 2, 1), jnp.stack(tri_list)
 
     return jax.shard_map(local_step, mesh=mesh, in_specs=(mat_spec,), out_specs=(mat_spec, P("part"), P(None, ("part", "row"), None), P("part")), check_vma=False)

time: 975 us -> 926 us (0.950)
  Pallas kernels: 789 us -> 748 us
    pallas_call x4, Pallas kernels: 286 us -> 232 us  [times_matrix(): pl.pallas_call(av_kernel, grid_spec=pltpu.PrefetchScalarGridSpec(num_scal...]
    pallas_call x4 -> x5, Pallas kernels: 26.2 us -> 38.3 us  [the longest x4 35.7 us: place(): pl.pallas_call(place_kernel, grid_spec=pltpu.PrefetchScalarGridSpec(num_s...]
    psum x4, waiting for transfers between devices: 103 us -> 91.7 us  [local_step(): z = lax.psum(z_part, ('col', 'row'))]
    ppermute x2, waiting for transfers between devices: 16.1 us -> 26.2 us  [first_panels(): got = lax.ppermute(jnp.where(left, high, low), 'col', [(0, 1), (1, 0)])]
  transfers between devices with their start and end apart: 10 -> 10, of which waited for: 7 -> 6; matrix products, arithmetic and copies ran while one was open for 1% -> 1% of each run, Pallas kernels for 51% -> 50%
where the time goes in v3:
time: 926 us; the launch traced here: 922 us
  Pallas kernels  748 us (81%)
  waiting for transfers between devices  146 us (16%)
  between operations  14.3 us (2%)
    pallas_call x4, Pallas kernels, times_matrix(): pl.pallas_call(av_kernel, grid_spec=pltpu.PrefetchScalarGridSpec(num_scal...  232 us
    pallas_call x4, Pallas kernels, panel_qr(): pl.pallas_call(functools.partial(qr_kernel, k), out_shape=(jax.ShapeDtype...  148 us
    pallas_call x1, Pallas kernels, final_update(): pl.pallas_call(final_kernel, grid_spec=pltpu.PrefetchScalarGridSpec(num_s...  144 us
    psum x4, waiting for transfers between devices, local_step(): z = lax.psum(z_part, ('col', 'row'))  91.7 us
    pallas_call x3, Pallas kernels, ahead(): pl.pallas_call(functools.partial(ahead_kernel, k), grid=(2, NW), in_specs...  88.3 us
    pallas_call x4, Pallas kernels, make_w(): pl.pallas_call(functools.partial(w_kernel, k), out_shape=tuple(outs), scr...  77.6 us
    pallas_call x4, Pallas kernels, place(): pl.pallas_call(place_kernel, grid_spec=pltpu.PrefetchScalarGridSpec(num_s...  35.7 us
    all_gather x4, waiting for transfers between devices, first_panels(): out.append(interleave(lax.all_gather(mine, everyone)))  26.4 us
  transfers between devices with their start and end apart: 10, of which 6 were waited for; matrix products, arithmetic and copies ran while one was open for 1% of the time, Pallas kernels for 50%

profile of v3, /device:TPU:0, one launch (start us, length us, event | category | flops | bytes accessed | tf_op | source)
XLA Modules:
  0.0 921.9 jit_solution(252408372581994053)
XLA Ops:
  7.2 2.6 first_columns.1
  9.8 1.5 slice_bitcast_fusion
  11.4 3.4 collective-permute-start
  14.7 9.1 collective-permute-done
  23.9 0.9 broadcast_select_fusion.2
  24.8 0.0 all-gather.11.cloned.1.call-start
  24.9 0.7 all-gather.11.cloned.1.call-update
  25.6 0.6 pad_add_fusion.pq_ref
  26.2 26.3 %all-gather.9.cloned.1.call-done = f32[512,1536]{1,0:T(8,128)} async-done(((f32[64,1536]{1,0:T(8,128)}), f32[512,1536]{1,0:T(8,128)}) %all-gather.9.cloned.1.call-update) | async-done | bytes 3145744 | tf_op jit(solution)/shard_map/all_gather | solution.py:630
  52.5 4.6 interleave.4.p_ref
  57.1 37.1 %panel_qr0.1 = (bf16[192,12288]{1,0:T(8,128)(2,1)}, f32[128,64]{1,0:T(8,128)}, f32[64,64]{1,0:T(8,128)}) custom-call(f32[64,12288]{1,0:T(8,128)} %interleave.4.p_ref), custom_call_target="tpu_custom_call" | custom-call | flops 200000000 | bytes 200000 | tf_op jit(solution)/shard_map/panel_qr0/pallas_call | solution.py:218
  94.2 58.1 %times_matrix.4 = (f32[64,12288]{1,0:T(8,128)}, f32[64,3072]{1,0:T(8,128)}) custom-call(s32[21]{0:T(128)} %constant.17.clone.ti_ref, s32[21]{0:T(128)} %constant.18.clone.tj_ref, s32[2]{0:T(128)} %pad_add_fusion.pq_ref, f32[3072,6144]{1,0:T(8,128)} %bitcast.2.l_ref, bf16[192,12288]{1,0:T(8,128)(2,1)} %get-tuple-element.45.vtc_ref.vtp_ref.refs_1_.refs_3_.refs_5_.a_ref.ac_ref, ...), custom_call_target="tpu_custom_call" | custom-call | flops 400000000 | bytes 400000 | tf_op jit(solution)/shard_map/times_matrix/pallas_call | solution.py:324
  152.3 0.0 all-gather.13.cloned.1.call-start
  152.4 1.4 collective-permute-start.1
  153.8 17.1 %collective-permute-done.1 = f32[64,1536]{1,0:T(8,128)S(1)} collective-permute-done((f32[64,1536]{1,0:T(8,128)S(1)}, f32[64,1536]{1,0:T(8,128)S(1)}, u32[]{:S(2)}, u32[]{:S(2)}) %collective-permute-start.1) | collective-permute-done | bytes 393248 | tf_op jit(solution)/shard_map/ppermute | solution.py:628
  170.9 1.0 broadcast_select_fusion
  171.9 0.0 all-reduce.7.cloned.1.call-start
  172.0 4.6 interleave.5.refs_3_
  176.6 40.3 %all-reduce.5.cloned.1.call-done.refs_0_ = f32[64,12288]{1,0:T(8,128)} async-done(((f32[64,12288]{1,0:T(8,128)}), f32[64,12288]{1,0:T(8,128)}) %all-reduce.5.cloned.1.call-update) | async-done | bytes 3145744 | tf_op jit(solution)/shard_map/psum | solution.py:647
  216.9 20.2 %make_w0.1 = (bf16[192,12288]{1,0:T(8,128)(2,1)}, f32[64,12288]{1,0:T(8,128)}) custom-call(f32[64,12288]{1,0:T(8,128)} %all-reduce.5.cloned.1.call-done.refs_0_, bf16[192,12288]{1,0:T(8,128)(2,1)} %get-tuple-element.45.vtc_ref.vtp_ref.refs_1_.refs_3_.refs_5_.a_ref.ac_ref, f32[64,64]{1,0:T(8,128)} %get-tuple-element.47.refs_2_, f32[64,12288]{1,0:T(8,128)} %interleave.5.refs_3_), custom_call_target="tpu_custom_call" | custom-call | flops 100000000 | bytes 100000 | tf_op jit(solution)/shard_map/make_w0/pallas_call | solution.py:488
  237.1 37.1 %panel_qr1.1 = (bf16[192,12288]{1,0:T(8,128)(2,1)}, f32[128,64]{1,0:T(8,128)}, f32[64,64]{1,0:T(8,128)}) custom-call(f32[64,12288]{1,0:T(8,128)} %get-tuple-element.48.p_ref), custom_call_target="tpu_custom_call" | custom-call | flops 200000000 | bytes 200000 | tf_op jit(solution)/shard_map/panel_qr1/pallas_call | solution.py:218
  274.2 58.1 %times_matrix.5 = (f32[64,12288]{1,0:T(8,128)}, f32[64,3072]{1,0:T(8,128)}) custom-call(s32[21]{0:T(128)} %constant.17.clone.ti_ref, s32[21]{0:T(128)} %constant.18.clone.tj_ref, s32[2]{0:T(128)} %pad_add_fusion.pq_ref, f32[3072,6144]{1,0:T(8,128)} %bitcast.2.l_ref, ...), custom_call_target="tpu_custom_call" | custom-call | flops 400000000 | bytes 400000 | tf_op jit(solution)/shard_map/times_matrix/pallas_call | solution.py:324
  332.3 0.0 all-gather.15.cloned.1.call-start
  332.4 0.5 all-gather.15.cloned.1.call-update
  332.9 0.2 all-reduce.9.cloned.1.call-start
  333.1 4.6 interleave.6.refs_5_
  337.8 24.9 %ahead1.1 = (f32[64,12288]{1,0:T(8,128)}, f32[64,12288]{1,0:T(8,128)}) custom-call(bf16[192,12288]{1,0:T(8,128)(2,1)} %get-tuple-element.49.vtc_ref.vtp_ref.refs_0_.refs_1_.refs_3_.refs_7_.b_ref.bc_ref, bf16[192,12288]{1,0:T(8,128)(2,1)} %get-tuple-element.45.vtc_ref.vtp_ref.refs_1_.refs_3_.refs_5_.a_ref.ac_ref, ...), custom_call_target="tpu_custom_call" | custom-call | flops 100000000 | bytes 100000 | tf_op jit(solution)/shard_map/ahead1/pallas_call | solution.py:417
  362.7 27.8 %all-reduce.7.cloned.1.call-done.refs_0_ = f32[64,12288]{1,0:T(8,128)} async-done(((f32[64,12288]{1,0:T(8,128)}), f32[64,12288]{1,0:T(8,128)}) %all-reduce.7.cloned.1.call-update) | async-done | bytes 3145744 | tf_op jit(solution)/shard_map/psum | solution.py:647
  390.5 21.2 %make_w1.1 = (bf16[192,12288]{1,0:T(8,128)(2,1)}, f32[64,12288]{1,0:T(8,128)}) custom-call(f32[64,12288]{1,0:T(8,128)} %all-reduce.7.cloned.1.call-done.refs_0_, bf16[192,12288]{1,0:T(8,128)(2,1)} %get-tuple-element.49.vtc_ref.vtp_ref.refs_0_.refs_1_.refs_3_.refs_7_.b_ref.bc_ref, f32[64,64]{1,0:T(8,128)} %get-tuple-element.51.refs_2_, ...), custom_call_target="tpu_custom_call" | custom-call | flops 100000000 | bytes 100000 | tf_op jit(solution)/shard_map/make_w1/pallas_call | solution.py:488
  411.7 37.1 %panel_qr2.1 = (bf16[192,12288]{1,0:T(8,128)(2,1)}, f32[128,64]{1,0:T(8,128)}, f32[64,64]{1,0:T(8,128)}) custom-call(f32[64,12288]{1,0:T(8,128)} %get-tuple-element.56.p_ref), custom_call_target="tpu_custom_call" | custom-call | flops 200000000 | bytes 200000 | tf_op jit(solution)/shard_map/panel_qr2/pallas_call | solution.py:218
  448.8 58.1 %times_matrix.6 = (f32[64,12288]{1,0:T(8,128)}, f32[64,3072]{1,0:T(8,128)}) custom-call(s32[21]{0:T(128)} %constant.17.clone.ti_ref, s32[21]{0:T(128)} %constant.18.clone.tj_ref, s32[2]{0:T(128)} %pad_add_fusion.pq_ref, f32[3072,6144]{1,0:T(8,128)} %bitcast.2.l_ref, bf16[192,12288]{1,0:T(8,128)(2,1)} %get-tuple-element.57.vtc_ref.vtp_ref.refs_0_.refs_1_.refs_5_.a_ref.ac_ref, ...), custom_call_target="tpu_custom_call" | custom-call | flops 400000000 | bytes 400000 | tf_op jit(solution)/shard_map/times_matrix/pallas_call | solution.py:324
  507.0 0.0 all-reduce.11.cloned.1.call-start
  507.0 4.6 interleave.7.refs_9_
  511.7 30.0 %ahead2.1 = (f32[64,12288]{1,0:T(8,128)}, f32[64,12288]{1,0:T(8,128)}) custom-call(bf16[192,12288]{1,0:T(8,128)(2,1)} %get-tuple-element.57.vtc_ref.vtp_ref.refs_0_.refs_1_.refs_5_.a_ref.ac_ref, bf16[192,12288]{1,0:T(8,128)(2,1)} %get-tuple-element.45.vtc_ref.vtp_ref.refs_1_.refs_3_.refs_5_.a_ref.ac_ref, ...), custom_call_target="tpu_custom_call" | custom-call | flops 200000000 | bytes 200000 | tf_op jit(solution)/shard_map/ahead2/pallas_call | solution.py:417
  541.7 23.5 %all-reduce.9.cloned.1.call-done.refs_0_ = f32[64,12288]{1,0:T(8,128)} async-done(((f32[64,12288]{1,0:T(8,128)}), f32[64,12288]{1,0:T(8,128)}) %all-reduce.9.cloned.1.call-update) | async-done | bytes 3145744 | tf_op jit(solution)/shard_map/psum | solution.py:647
  565.2 21.1 %make_w2.1 = (bf16[192,12288]{1,0:T(8,128)(2,1)}, f32[64,12288]{1,0:T(8,128)}) custom-call(f32[64,12288]{1,0:T(8,128)} %all-reduce.9.cloned.1.call-done.refs_0_, bf16[192,12288]{1,0:T(8,128)(2,1)} %get-tuple-element.57.vtc_ref.vtp_ref.refs_0_.refs_1_.refs_5_.a_ref.ac_ref, f32[64,64]{1,0:T(8,128)} %get-tuple-element.59.refs_2_, ...), custom_call_target="tpu_custom_call" | custom-call | flops 100000000 | bytes 100000 | tf_op jit(solution)/shard_map/make_w2/pallas_call | solution.py:488
  586.3 37.1 %panel_qr3.1 = (bf16[192,12288]{1,0:T(8,128)(2,1)}, f32[128,64]{1,0:T(8,128)}, f32[64,64]{1,0:T(8,128)}) custom-call(f32[64,12288]{1,0:T(8,128)} %get-tuple-element.64.p_ref), custom_call_target="tpu_custom_call" | custom-call | flops 200000000 | bytes 200000 | tf_op jit(solution)/shard_map/panel_qr3/pallas_call | solution.py:218
  623.4 58.1 %times_matrix.7 = (f32[64,12288]{1,0:T(8,128)}, f32[64,3072]{1,0:T(8,128)}) custom-call(s32[21]{0:T(128)} %constant.17.clone.ti_ref, s32[21]{0:T(128)} %constant.18.clone.tj_ref, s32[2]{0:T(128)} %pad_add_fusion.pq_ref, f32[3072,6144]{1,0:T(8,128)} %bitcast.2.l_ref, bf16[192,12288]{1,0:T(8,128)(2,1)} %get-tuple-element.65.vtc_ref.vtp_ref.refs_0_.refs_1_.b_ref.bc_ref, ...), custom_call_target="tpu_custom_call" | custom-call | flops 400000000 | bytes 400000 | tf_op jit(solution)/shard_map/times_matrix/pallas_call | solution.py:324
  681.6 9.0 place.4
  690.7 0.8 copy.20
  691.4 8.8 place.5
  700.3 8.9 place.6
  709.2 33.4 %ahead3.1.refs_3_ = f32[64,12288]{1,0:T(8,128)} custom-call(bf16[192,12288]{1,0:T(8,128)(2,1)} %get-tuple-element.65.vtc_ref.vtp_ref.refs_0_.refs_1_.b_ref.bc_ref, bf16[192,12288]{1,0:T(8,128)(2,1)} %get-tuple-element.45.vtc_ref.vtp_ref.refs_1_.refs_3_.refs_5_.a_ref.ac_ref, bf16[192,12288]{1,0:T(8,128)(2,1)} %get-tuple-element.52.refs_2_.refs_4_.refs_6_.a_ref.ac_ref, ...), custom_call_target="tpu_custom_call" | custom-call | flops 300000000 | bytes 300000 | tf_op jit(solution)/shard_map/ahead3/pallas_call | solution.py:417
  742.6 0.7 pad_maximum_fusion.1
  743.2 3.4 maximum_bitcast_fusion
  746.6 15.2 %make_w3.1.b_ref.bc_ref = bf16[192,12288]{1,0:T(8,128)(2,1)} custom-call(f32[64,12288]{1,0:T(8,128)} %all-reduce.11.cloned.1.call-done.refs_0_, bf16[192,12288]{1,0:T(8,128)(2,1)} %get-tuple-element.65.vtc_ref.vtp_ref.refs_0_.refs_1_.b_ref.bc_ref, f32[64,64]{1,0:T(8,128)} %get-tuple-element.67.refs_2_, f32[64,12288]{1,0:T(8,128)} %ahead3.1.refs_3_), custom_call_target="tpu_custom_call" | custom-call | flops 100000000 | bytes 100000 | tf_op jit(solution)/shard_map/make_w3/pallas_call | solution.py:488
  761.8 9.0 place.7
  770.8 144.3 %final_update.1 = f32[3072,6144]{1,0:T(8,128)} custom-call(s32[4,36]{1,0:T(4,128)} %constant.19.clone.tab_ref, s32[2]{0:T(128)} %pad_add_fusion.pq_ref, f32[3072,6144]{1,0:T(8,128)} %bitcast.2.l_ref, bf16[3,3072,512]{2,1,0:T(8,128)(2,1)} %get-tuple-element.74.x_ref, bf16[3,512,6144]{2,1,0:T(8,128)(2,1)} %get-tuple-element.75.y_ref), custom_call_target="tpu_custom_call" | custom-call | flops 2000000000 | bytes 2000000 | tf_op jit(solution)/shard_map/final_update/pallas_call | solution.py:579
  (35 shorter events, 0.4 us)
Async XLA Ops:
  7.2 45.4 %all-gather.9.cloned.1.call-start = ((), (), s32[]{:S(2)}) async-start(), calls=%async_computation.4 | async-start | bytes 3538944 | tf_op jit(solution)/shard_map/all_gather | solution.py:630
  11.4 12.5 %collective-permute-start = (f32[64,1536]{1,0:T(8,128)S(1)}, f32[64,1536]{1,0:T(8,128)S(1)}, u32[]{:S(2)}, u32[]{:S(2)}) collective-permute-start(f32[64,1536]{1,0:T(8,128)S(1)} %slice_select_fusion), channel_id=1, source_target_pairs={{0,4},{4,0},{1,5},{5,1},{2,6},{6,2},{3,7},{7,3}} | collective-permute-start | bytes 1179656 | tf_op jit(solution)/shard_map/ppermute | solution.py:628
  24.8 147.1 %all-gather.11.cloned.1.call-start = ((), (), s32[]{:S(2)}) async-start(), calls=%async_computation.5 | async-start | bytes 3538944 | tf_op jit(solution)/shard_map/all_gather | solution.py:630
  25.6 191.3 %all-reduce.5.cloned.1.call-start = ((), (), s32[]{:S(2)}) async-start(), calls=%async_computation | async-start | bytes 6291456 | tf_op jit(solution)/shard_map/psum | solution.py:647
  152.3 180.8 %all-gather.13.cloned.1.call-start = ((), (), s32[]{:S(2)}) async-start(), calls=%async_computation.6 | async-start | bytes 3538944 | tf_op jit(solution)/shard_map/all_gather | solution.py:630
  152.4 18.4 %collective-permute-start.1 = (f32[64,1536]{1,0:T(8,128)S(1)}, f32[64,1536]{1,0:T(8,128)S(1)}, u32[]{:S(2)}, u32[]{:S(2)}) collective-permute-start(f32[64,1536]{1,0:T(8,128)S(1)} %slice_select_fusion.2), channel_id=1, source_target_pairs={{0,4},{4,0},{1,5},{5,1},{2,6},{6,2},{3,7},{7,3}} | collective-permute-start | bytes 1179656 | tf_op jit(solution)/shard_map/ppermute | solution.py:628
  171.9 218.6 %all-reduce.7.cloned.1.call-start = ((), (), s32[]{:S(2)}) async-start(), calls=%async_computation.1 | async-start | bytes 6291456 | tf_op jit(solution)/shard_map/psum | solution.py:647
  332.3 174.7 %all-gather.15.cloned.1.call-start = ((), (), s32[]{:S(2)}) async-start(), calls=%async_computation.7 | async-start | bytes 3538944 | tf_op jit(solution)/shard_map/all_gather | solution.py:630
  332.9 232.3 %all-reduce.9.cloned.1.call-start = ((), (), s32[]{:S(2)}) async-start(), calls=%async_computation.2 | async-start | bytes 6291456 | tf_op jit(solution)/shard_map/psum | solution.py:647
  507.0 239.7 %all-reduce.11.cloned.1.call-start = ((), (), s32[]{:S(2)}) async-start(), calls=%async_computation.3 | async-start | bytes 6291456 | tf_op jit(solution)/shard_map/psum | solution.py:647
  681.5 9.1 copy-start.6
  681.5 9.1 copy-start.7
  681.6 9.0 copy-start.8
  681.6 9.0 copy-start.9
  709.1 33.4 %copy-start.2 = (f32[64,64]{1,0:T(8,128)S(1)}, f32[64,64]{1,0:T(8,128)}, u32[]{:S(2)}) copy-start(f32[64,64]{1,0:T(8,128)} %get-tuple-element.47.refs_2_) | copy-start | bytes 49156
  709.1 33.4 %copy-start.3 = (f32[64,64]{1,0:T(8,128)S(1)}, f32[64,64]{1,0:T(8,128)}, u32[]{:S(2)}) copy-start(f32[64,64]{1,0:T(8,128)} %get-tuple-element.51.refs_2_) | copy-start | bytes 49156
  709.1 33.4 %copy-start.4 = (f32[64,64]{1,0:T(8,128)S(1)}, f32[64,64]{1,0:T(8,128)}, u32[]{:S(2)}) copy-start(f32[64,64]{1,0:T(8,128)} %get-tuple-element.59.refs_2_) | copy-start | bytes 49156
  709.1 33.4 %copy-start.5 = (f32[64,64]{1,0:T(8,128)S(1)}, f32[64,64]{1,0:T(8,128)}, u32[]{:S(2)}) copy-start(f32[64,64]{1,0:T(8,128)} %get-tuple-element.67.refs_2_) | copy-start | bytes 49156
  709.2 34.1 %copy-start = (f32[64,3072]{1,0:T(8,128)S(1)}, f32[64,3072]{1,0:T(8,128)}, u32[]{:S(2)}) copy-start(f32[64,3072]{1,0:T(8,128)} %get-tuple-element.80) | copy-start | bytes 2359300
  709.2 34.1 %copy-start.1 = (f32[64,3072]{1,0:T(8,128)S(1)}, f32[64,3072]{1,0:T(8,128)}, u32[]{:S(2)}) copy-start(f32[64,3072]{1,0:T(8,128)} %get-tuple-element.81) | copy-start | bytes 2359300
Sparse Core Ops, SparseCore 0:
  25.0 27.5 all-gather.8
  54.3 26.3 all-gather.10
  152.4 64.4 all-reduce.4
  218.6 26.4 all-gather.12
  332.4 58.0 all-reduce.6
  392.2 26.4 all-gather.14
  507.1 58.0 all-reduce.8
  681.7 58.0 all-reduce.10
